TPU v7x, 32 devices: a whole 2x2x4 slice. The times are simulated.
32 devices in a mesh: dp: 8 (over z, y), tensor: 4 (over x, core).
Axes of the slice: x: 2, y: 2, z: 4, core: 2. Of those that a mesh axis runs over, the one named last changes fastest.
Arguments:
- inputs: float32 [12288, 768], P(('dp', 'tensor')), may hold values from -40 to 40
- cotangent: float32 [12288, 768], P(('dp', 'tensor')), may hold values from -12 to 12
- clip_lengths: int32 [12], replicated, may hold values from 1 to 1500, 12288 in all
- inward_weight: float32 [768, 3, 768], P('dp', None, 'tensor'), may hold values from -0.5 to 0.5
- outward_weight: float32 [768, 768], P('tensor', 'dp'), may hold values from -0.875 to 0.875
- expand_weight: float32 [768, 3072], P('dp', 'tensor'), may hold values from -0.21875 to 0.21875
- shrink_weight: float32 [3072, 768], P('tensor', 'dp'), may hold values from -0.109375 to 0.109375
- gains: float32 [2, 768], P(None, ('dp', 'tensor')), may hold values from 0.5 to 1.5
- shifts: float32 [2, 768], P(None, ('dp', 'tensor')), may hold values from -1.75 to 1.75
- biases: float32 [4, 768], P(None, ('dp', 'tensor')), may hold values from -1.75 to 1.75
- expand_bias: float32 [3072], P(('dp', 'tensor')), may hold values from -1.75 to 1.75
- inward_moment: float32 [768, 3, 768], P('dp', None, 'tensor'), may hold values from -199.53225 to 199.53225
- outward_moment: float32 [768, 768], P('tensor', 'dp'), may hold values from -199.53225 to 199.53225
- expand_moment: float32 [768, 3072], P('dp', 'tensor'), may hold values from -199.53225 to 199.53225
- shrink_moment: float32 [3072, 768], P('tensor', 'dp'), may hold values from -199.53225 to 199.53225
- gains_moment: float32 [2, 768], P(None, ('dp', 'tensor')), may hold values from -128 to 128
- shifts_moment: float32 [2, 768], P(None, ('dp', 'tensor')), may hold values from -128 to 128
- biases_moment: float32 [4, 768], P(None, ('dp', 'tensor')), may hold values from -128 to 128
- expand_bias_moment: float32 [3072], P(('dp', 'tensor')), may hold values from -128 to 128
Outputs:
- output: float32 [12288, 768], P(('dp', 'tensor'))
- input_grad: float32 [12288, 768], P(('dp', 'tensor'))
- inward_grad: float32 [768, 3, 768], P('dp', None, 'tensor')
- outward_grad: float32 [768, 768], P('tensor', 'dp')
- expand_grad: float32 [768, 3072], P('dp', 'tensor')
- shrink_grad: float32 [3072, 768], P('tensor', 'dp')
- gains_grad: float32 [2, 768], P(None, ('dp', 'tensor'))
- shifts_grad: float32 [2, 768], P(None, ('dp', 'tensor'))
- biases_grad: float32 [4, 768], P(None, ('dp', 'tensor'))
- expand_bias_grad: float32 [3072], P(('dp', 'tensor'))
- inward_new: float32 [768, 3, 768], P('dp', None, 'tensor')
- outward_new: float32 [768, 768], P('tensor', 'dp')
- expand_new: float32 [768, 3072], P('dp', 'tensor')
- shrink_new: float32 [3072, 768], P('tensor', 'dp')
- gains_new: float32 [2, 768], P(None, ('dp', 'tensor'))
- shifts_new: float32 [2, 768], P(None, ('dp', 'tensor'))
- biases_new: float32 [4, 768], P(None, ('dp', 'tensor'))
- expand_bias_new: float32 [3072], P(('dp', 'tensor'))
- inward_state: float32 [768, 3, 768], P('dp', None, 'tensor')
- outward_state: float32 [768, 768], P('tensor', 'dp')
- expand_state: float32 [768, 3072], P('dp', 'tensor')
- shrink_state: float32 [3072, 768], P('tensor', 'dp')
- gains_state: float32 [2, 768], P(None, ('dp', 'tensor'))
- shifts_state: float32 [2, 768], P(None, ('dp', 'tensor'))
- biases_state: float32 [4, 768], P(None, ('dp', 'tensor'))
- expand_bias_state: float32 [3072], P(('dp', 'tensor'))
Inputs may be any that keep to these rules, and one draw needn't show every extreme that they name: `clip_lengths`: clips lie end to end in token order and together fill all 12288 tokens; the longest has exactly 1500 frames.
All inputs are finite; a program needn't handle non-finite values.
Results may differ from a plain program's by a relative error of at most 0.033.
Values may be sent and summed in bfloat16 or wider, within the bound.
A program may use at most 256 MiB of HBM per device.

v0:
```python
import math

import jax
import jax.numpy as jnp
from jax import lax
from jax.sharding import PartitionSpec as P

HDIM = 64
MAXCLIP = 1500
NS_STEPS = 3


norm_epsilon = 1e-05
frobenius_epsilon = 1e-07
quintic_one = 3.4445
quintic_two = -4.775
quintic_three = 2.0315
momentum_decay = 0.9
learn_rate = 0.2
vector_rate = 0.003
masked_score = -1e30
root_half = 0.7071067811865476
gauss_factor = 0.3989422804014327


def padded(cells, sides, width):
    for axis, dim in sides:
        count = lax.axis_size(axis)
        ends = count - 1
        head = lax.slice_in_dim(cells, 0, width, axis=dim)
        tail = lax.slice_in_dim(cells, cells.shape[dim] - width, cells.shape[dim], axis=dim)
        cells = jnp.concatenate(
            [
                lax.ppermute(tail, axis, [(i, (i + 1) % count) for i in range(ends)]),
                cells,
                lax.ppermute(head, axis, [((i + 1) % count, i) for i in range(ends)]),
            ],
            axis=dim,
        )
    return cells


def from_root(value, axis, source):
    kept = jnp.where(lax.axis_index(axis) == source, value, 0).astype(value.dtype)
    return lax.psum(kept, axis)


def normalize(values_in):
    center = values_in - jnp.mean(values_in, axis=-1, keepdims=True)
    inverse = lax.rsqrt(jnp.mean(center * center, axis=-1, keepdims=True) + norm_epsilon)
    return (center * inverse, inverse)


def norm_back(grad_rows, unit, inverse, gain):
    scaled = grad_rows * gain
    return inverse * (
        scaled
        - jnp.mean(scaled, axis=-1, keepdims=True)
        - unit * jnp.mean(scaled * unit, axis=-1, keepdims=True)
    )


def gelu_value(pre):
    return pre * 0.5 * (1.0 + lax.erf(pre * root_half))


def gelu_slope(pre):
    return 0.5 * (1.0 + lax.erf(pre * root_half)) + pre * jnp.exp(-0.5 * pre * pre) * gauss_factor


def clip_index(clip_lengths, positions, total):
    ends = jnp.cumsum(clip_lengths, dtype=jnp.int32)
    found = jnp.sum(
        (ends[None, :] <= positions[:, None]).astype(jnp.int32), axis=1, dtype=jnp.int32
    )
    inside = (positions >= 0) & (positions < total)
    return jnp.where(inside, found, -1)


def orthogonalize(matrix):
    wide = lax.optimization_barrier(matrix).astype(jnp.float32)
    state = (wide / (jnp.sqrt(jnp.sum(wide * wide)) + frobenius_epsilon)).astype(jnp.bfloat16)
    for sweep in range(NS_STEPS):
        gram = jnp.dot(state, state.T, preferred_element_type=jnp.float32).astype(jnp.bfloat16)
        poly = (
            quintic_two * lax.optimization_barrier(gram).astype(jnp.float32)
            + quintic_three * jnp.dot(gram, gram, preferred_element_type=jnp.float32)
        ).astype(jnp.bfloat16)
        state = (
            quintic_one * lax.optimization_barrier(state).astype(jnp.float32)
            + jnp.dot(poly, state, preferred_element_type=jnp.float32)
        ).astype(jnp.bfloat16)
    return state


def contract_first(left, right):
    return lax.dot_general(
        left, right, (((0,), (0,)), ((), ())), preferred_element_type=jnp.float32
    )


def contract_last(left, right):
    return lax.dot_general(
        left, right, (((1,), (1,)), ((), ())), preferred_element_type=jnp.float32
    )


def gather_rows(block):
    return lax.all_gather(block, "tensor", axis=0, tiled=True)


def sum_rows(producer, count):
    return lax.psum_scatter(
        producer(jnp.int32(0), count * lax.axis_size("tensor")),
        "tensor",
        scatter_dimension=0,
        tiled=True,
    )


def join_inward(pieces, data_count, tensor_count, width):
    grid = pieces.reshape(data_count, tensor_count, width // data_count, 3, width // tensor_count)
    return grid.transpose(0, 2, 3, 1, 4).reshape(width, 3 * width)


def split_inward(matrix, data_count, tensor_count, width):
    grid = matrix.reshape(data_count, width // data_count, 3, tensor_count, width // tensor_count)
    return grid.transpose(0, 3, 1, 2, 4).reshape(data_count * tensor_count, -1)


def join_rowsplit(pieces, data_count, tensor_count, height, width):
    grid = pieces.reshape(data_count, tensor_count, height // data_count, width // tensor_count)
    return grid.transpose(0, 2, 1, 3).reshape(height, width)


def split_rowsplit(matrix, data_count, tensor_count, height, width):
    grid = matrix.reshape(data_count, height // data_count, tensor_count, width // tensor_count)
    return grid.transpose(0, 2, 1, 3).reshape(data_count * tensor_count, -1)


def join_colsplit(pieces, data_count, tensor_count, height, width):
    grid = pieces.reshape(data_count, tensor_count, height // tensor_count, width // data_count)
    return grid.transpose(1, 2, 0, 3).reshape(height, width)


def split_colsplit(matrix, data_count, tensor_count, height, width):
    grid = matrix.reshape(tensor_count, height // tensor_count, data_count, width // data_count)
    return grid.transpose(2, 0, 1, 3).reshape(data_count * tensor_count, -1)


def local(
    inputs,
    cotangent,
    clip_lengths,
    inward_weight,
    outward_weight,
    expand_weight,
    shrink_weight,
    gains,
    shifts,
    biases,
    expand_bias,
    inward_moment,
    outward_moment,
    expand_moment,
    shrink_moment,
    gains_moment,
    shifts_moment,
    biases_moment,
    expand_bias_moment,
):
    data_count = lax.axis_size("dp")
    tensor_count = lax.axis_size("tensor")
    devices = data_count * tensor_count
    data_at = lax.axis_index("dp")
    tensor_at = lax.axis_index("tensor")
    rows = inputs.shape[0]
    width = inputs.shape[1]
    run = rows * tensor_count
    total = run * data_count
    head_cols = inward_weight.shape[2]
    hidden_cols = expand_weight.shape[1]
    hidden_width = hidden_cols * tensor_count
    local_heads = head_cols // HDIM
    scale = 1.0 / math.sqrt(HDIM)
    block_rows = min(512, run)
    block_count = run // block_rows
    window = block_rows + 2 * MAXCLIP
    full_gains, full_shifts, full_biases, full_hidden = (
        lax.all_gather(gains, ("dp", "tensor"), axis=1, tiled=True),
        lax.all_gather(shifts, ("dp", "tensor"), axis=1, tiled=True),
        lax.all_gather(biases, ("dp", "tensor"), axis=1, tiled=True),
        lax.all_gather(expand_bias, ("dp", "tensor"), axis=0, tiled=True),
    )
    inward_full, outward_full, expand_full, shrink_full = (
        lax.all_gather(inward_weight.astype(jnp.bfloat16), "dp", axis=0, tiled=True),
        lax.all_gather(outward_weight.astype(jnp.bfloat16), "dp", axis=1, tiled=True),
        lax.all_gather(expand_weight.astype(jnp.bfloat16), "dp", axis=0, tiled=True),
        lax.all_gather(shrink_weight.astype(jnp.bfloat16), "dp", axis=1, tiled=True),
    )
    inward_flat = inward_full.reshape(width, 3 * head_cols)
    bias_query = lax.dynamic_slice_in_dim(full_biases[0], tensor_at * head_cols, head_cols)
    bias_value = lax.dynamic_slice_in_dim(full_biases[1], tensor_at * head_cols, head_cols)
    bias_hidden = lax.dynamic_slice_in_dim(full_hidden, tensor_at * hidden_cols, hidden_cols)
    start_pos = data_at * run
    query_tags = clip_index(clip_lengths, start_pos + lax.iota(jnp.int32, run), total)
    key_tags = clip_index(
        clip_lengths, start_pos - MAXCLIP + lax.iota(jnp.int32, run + 2 * MAXCLIP), total
    )
    unit_one, inverse_one = normalize(inputs)
    rows_one = gather_rows((unit_one * full_gains[0] + full_shifts[0]).astype(jnp.bfloat16))
    mixed = jnp.dot(rows_one, inward_flat, preferred_element_type=jnp.float32).reshape(
        run, 3, head_cols
    )
    query = (mixed[:, 0] + bias_query).astype(jnp.bfloat16)
    pairs = jnp.concatenate(
        [mixed[:, 1].astype(jnp.bfloat16), (mixed[:, 2] + bias_value).astype(jnp.bfloat16)], axis=1
    )
    extended = padded(pairs, (("dp", 0),), MAXCLIP)

    def block_inputs(block):
        start = block * block_rows
        query_rows = lax.dynamic_slice_in_dim(query, start, block_rows, 0)
        pair_rows = lax.dynamic_slice_in_dim(extended, start, window, 0)
        allowed = (
            lax.dynamic_slice_in_dim(query_tags, start, block_rows)[:, None]
            == lax.dynamic_slice_in_dim(key_tags, start, window)[None, :]
        )
        return (start, query_rows, pair_rows, allowed)

    def head_scores(query_rows, pair_rows, allowed, head):
        offset = head * HDIM
        query_head = query_rows[:, offset : offset + HDIM]
        key_head = pair_rows[:, offset : offset + HDIM]
        value_head = pair_rows[:, head_cols + offset : head_cols + offset + HDIM]
        score = jnp.where(allowed, contract_last(query_head, key_head) * scale, masked_score)
        return (query_head, key_head, value_head, score)

    def forward_block(carry, block):
        start, query_rows, pair_rows, allowed = block_inputs(block)
        outputs = []
        totals = []
        for head in range(local_heads):
            query_head, key_head, value_head, score = head_scores(
                query_rows, pair_rows, allowed, head
            )
            top = jnp.max(score, axis=1, keepdims=True)
            log_total = top + jnp.log(jnp.sum(jnp.exp(score - top), axis=1, keepdims=True))
            probs = jnp.exp(score - log_total).astype(jnp.bfloat16)
            outputs.append(
                jnp.dot(probs, value_head, preferred_element_type=jnp.float32).astype(jnp.bfloat16)
            )
            totals.append(log_total[:, 0])
        return (carry, (jnp.concatenate(outputs, axis=1), jnp.stack(totals, axis=0)))

    unused, (attended_blocks, total_blocks) = lax.scan(
        forward_block, jnp.zeros((), jnp.float32), lax.iota(jnp.int32, block_count)
    )
    attended = attended_blocks.reshape(run, head_cols)

    def attend_out(start, count):
        return jnp.dot(
            lax.dynamic_slice_in_dim(attended, start, count, 0),
            outward_full,
            preferred_element_type=jnp.float32,
        )

    mid = inputs + sum_rows(attend_out, rows) + full_biases[2]
    unit_two, inverse_two = normalize(mid)
    rows_two = gather_rows((unit_two * full_gains[1] + full_shifts[1]).astype(jnp.bfloat16))
    pre = jnp.dot(rows_two, expand_full, preferred_element_type=jnp.float32) + bias_hidden
    act = gelu_value(pre).astype(jnp.bfloat16)

    def feed_out(start, count):
        return jnp.dot(
            lax.dynamic_slice_in_dim(act, start, count, 0),
            shrink_full,
            preferred_element_type=jnp.float32,
        )

    output = mid + sum_rows(feed_out, rows) + full_biases[3]
    grad_full = gather_rows(cotangent.astype(jnp.bfloat16))
    pre_grad = contract_last(grad_full, shrink_full) * gelu_slope(pre)
    pre_grad_b = pre_grad.astype(jnp.bfloat16)
    shrink_part = contract_first(act, grad_full)
    expand_part = contract_first(rows_two, pre_grad_b)

    def feed_back(start, count):
        return contract_last(lax.dynamic_slice_in_dim(pre_grad_b, start, count, 0), expand_full)

    normed_two_grad = sum_rows(feed_back, rows)
    mid_grad = cotangent + norm_back(normed_two_grad, unit_two, inverse_two, full_gains[1])
    mid_full = gather_rows(mid_grad.astype(jnp.bfloat16))
    outward_part = contract_first(attended, mid_full)
    attended_grad = contract_last(mid_full, outward_full).astype(jnp.bfloat16)

    def backward_block(carry, inputs_now):
        block, log_totals = inputs_now
        start, query_rows, pair_rows, allowed = block_inputs(block)
        grad_rows = lax.dynamic_slice_in_dim(attended_grad, start, block_rows, 0)
        out_rows = lax.dynamic_slice_in_dim(attended, start, block_rows, 0)
        query_parts = []
        key_parts = []
        value_parts = []
        for head in range(local_heads):
            offset = head * HDIM
            query_head, key_head, value_head, score = head_scores(
                query_rows, pair_rows, allowed, head
            )
            exact = jnp.exp(score - log_totals[head][:, None])
            probs = exact.astype(jnp.bfloat16)
            grad_head = grad_rows[:, offset : offset + HDIM]
            delta = jnp.sum(
                grad_head.astype(jnp.float32)
                * out_rows[:, offset : offset + HDIM].astype(jnp.float32),
                axis=1,
            )
            prob_grad = contract_last(grad_head, value_head)
            score_grad = (exact * (prob_grad - delta[:, None])).astype(jnp.bfloat16)
            query_parts.append(
                jnp.dot(score_grad, key_head, preferred_element_type=jnp.float32) * scale
            )
            key_parts.append(contract_first(score_grad, query_head) * scale)
            value_parts.append(contract_first(probs, grad_head))
        update = jnp.concatenate(key_parts + value_parts, axis=1)
        current = lax.dynamic_slice_in_dim(carry, start, window, 0)
        carry = lax.dynamic_update_slice_in_dim(carry, current + update, start, 0)
        return (carry, jnp.concatenate(query_parts, axis=1))

    initial = jnp.zeros((run + 2 * MAXCLIP, 2 * head_cols), jnp.float32)
    pair_grads, query_blocks = lax.scan(
        backward_block, initial, (lax.iota(jnp.int32, block_count), total_blocks)
    )
    query_grad = query_blocks.reshape(run, head_cols)
    rims = jnp.concatenate([pair_grads[:MAXCLIP], pair_grads[MAXCLIP + run :]], axis=0)
    arrived = padded(rims.astype(jnp.bfloat16), (("dp", 0),), MAXCLIP).astype(rims.dtype)
    owned = pair_grads[MAXCLIP : MAXCLIP + run]
    owned = owned.at[:MAXCLIP].add(arrived[:MAXCLIP])
    owned = owned.at[run - MAXCLIP :].add(arrived[3 * MAXCLIP :])
    key_grad = owned[:, :head_cols]
    value_grad = owned[:, head_cols:]
    mixed_grad = (
        jnp.stack([query_grad, key_grad, value_grad], axis=1)
        .astype(jnp.bfloat16)
        .reshape(run, 3 * head_cols)
    )
    inward_part = contract_first(rows_one, mixed_grad).reshape(width, 3, head_cols)

    def attend_back(start, count):
        return contract_last(mixed_grad, inward_flat)

    normed_one_grad = sum_rows(attend_back, rows)
    input_grad = mid_grad + norm_back(normed_one_grad, unit_one, inverse_one, full_gains[0])
    inward_grad, outward_grad, expand_grad, shrink_grad = (
        lax.psum_scatter(inward_part, "dp", scatter_dimension=0, tiled=True),
        lax.psum_scatter(outward_part, "dp", scatter_dimension=1, tiled=True),
        lax.psum_scatter(expand_part, "dp", scatter_dimension=0, tiled=True),
        lax.psum_scatter(shrink_part, "dp", scatter_dimension=1, tiled=True),
    )
    empty_row = jnp.zeros((width,), jnp.float32)
    gains_part = jnp.stack(
        [jnp.sum(normed_one_grad * unit_one, axis=0), jnp.sum(normed_two_grad * unit_two, axis=0)]
    )
    shifts_part = jnp.stack([jnp.sum(normed_one_grad, axis=0), jnp.sum(normed_two_grad, axis=0)])
    biases_part = jnp.stack(
        [
            lax.dynamic_update_slice_in_dim(
                empty_row, jnp.sum(query_grad, axis=0), tensor_at * head_cols, 0
            ),
            lax.dynamic_update_slice_in_dim(
                empty_row, jnp.sum(value_grad, axis=0), tensor_at * head_cols, 0
            ),
            jnp.sum(mid_grad, axis=0),
            jnp.sum(cotangent, axis=0),
        ]
    )
    hidden_part = lax.dynamic_update_slice_in_dim(
        jnp.zeros((hidden_width,), jnp.float32),
        jnp.sum(pre_grad, axis=0),
        tensor_at * hidden_cols,
        0,
    )
    gains_grad, shifts_grad, biases_grad, expand_bias_grad = (
        lax.psum_scatter(gains_part, ("dp", "tensor"), scatter_dimension=1, tiled=True),
        lax.psum_scatter(shifts_part, ("dp", "tensor"), scatter_dimension=1, tiled=True),
        lax.psum_scatter(biases_part, ("dp", "tensor"), scatter_dimension=1, tiled=True),
        lax.psum_scatter(hidden_part, ("dp", "tensor"), scatter_dimension=0, tiled=True),
    )
    inward_state = momentum_decay * inward_moment + inward_grad
    outward_state = momentum_decay * outward_moment + outward_grad
    expand_state = momentum_decay * expand_moment + expand_grad
    shrink_state = momentum_decay * shrink_moment + shrink_grad
    gains_state = momentum_decay * gains_moment + gains_grad
    shifts_state = momentum_decay * shifts_moment + shifts_grad
    biases_state = momentum_decay * biases_moment + biases_grad
    expand_bias_state = momentum_decay * expand_bias_moment + expand_bias_grad
    flat_in = inward_state.astype(jnp.bfloat16).reshape(1, -1)
    flat_out = outward_state.astype(jnp.bfloat16).reshape(1, -1)
    flat_up = expand_state.astype(jnp.bfloat16).reshape(1, -1)
    flat_down = shrink_state.astype(jnp.bfloat16).reshape(1, -1)
    size_in = flat_in.shape[1]
    size_down = flat_down.shape[1]
    size_out = flat_out.shape[1]
    me = data_at * tensor_count + tensor_at
    whole_in, whole_out, whole_up, whole_down = (
        lax.all_gather(flat_in, ("dp", "tensor"), axis=0, tiled=True),
        lax.all_gather(flat_out, ("dp", "tensor"), axis=0, tiled=True),
        lax.all_gather(flat_up, ("dp", "tensor"), axis=0, tiled=True),
        lax.all_gather(flat_down, ("dp", "tensor"), axis=0, tiled=True),
    )

    def work_in():
        return split_inward(
            orthogonalize(join_inward(whole_in, data_count, tensor_count, width)),
            data_count,
            tensor_count,
            width,
        )

    def work_down():
        ortho_down = orthogonalize(
            join_colsplit(whole_down, data_count, tensor_count, hidden_width, width).T
        )
        return split_colsplit(ortho_down.T, data_count, tensor_count, hidden_width, width)

    def work_out():
        return split_colsplit(
            orthogonalize(join_colsplit(whole_out, data_count, tensor_count, width, width)),
            data_count,
            tensor_count,
            width,
            width,
        )

    def work_up():
        return split_rowsplit(
            orthogonalize(join_rowsplit(whole_up, data_count, tensor_count, width, hidden_width)),
            data_count,
            tensor_count,
            width,
            hidden_width,
        )

    def send_back(pieces, root):
        return from_root(pieces, ("dp", "tensor"), root)

    owner_second = devices // 2
    first_in, first_down = lax.cond(
        me == 0,
        lambda: (work_in(), work_down()),
        lambda: (jnp.zeros_like(whole_in), jnp.zeros_like(whole_down)),
    )
    second_out, second_up = lax.cond(
        me == owner_second,
        lambda: (work_out(), work_up()),
        lambda: (jnp.zeros_like(whole_out), jnp.zeros_like(whole_up)),
    )
    first_all = send_back(jnp.concatenate([first_in, first_down], axis=1), 0)
    second_all = send_back(jnp.concatenate([second_out, second_up], axis=1), owner_second)
    mine_first = lax.dynamic_index_in_dim(first_all, me, 0, keepdims=False)
    mine_second = lax.dynamic_index_in_dim(second_all, me, 0, keepdims=False)
    mine_in = mine_first[:size_in]
    mine_down = mine_first[size_in : size_in + size_down]
    mine_out = mine_second[:size_out]
    mine_up = mine_second[size_out:]
    ortho_in = mine_in.reshape(inward_weight.shape).astype(jnp.float32)
    ortho_down = mine_down.reshape(shrink_weight.shape).astype(jnp.float32)
    ortho_out = mine_out.reshape(outward_weight.shape).astype(jnp.float32)
    ortho_up = mine_up.reshape(expand_weight.shape).astype(jnp.float32)
    inward_new = inward_weight - learn_rate * 0.2 * math.sqrt(3 * width) * ortho_in
    outward_new = outward_weight - learn_rate * 0.2 * math.sqrt(width) * ortho_out
    expand_new = expand_weight - learn_rate * 0.2 * math.sqrt(max(width, hidden_width)) * ortho_up
    shrink_new = shrink_weight - learn_rate * 0.2 * math.sqrt(max(width, hidden_width)) * ortho_down
    gains_new = gains - vector_rate * gains_state
    shifts_new = shifts - vector_rate * shifts_state
    biases_new = biases - vector_rate * biases_state
    expand_bias_new = expand_bias - vector_rate * expand_bias_state
    return (
        output,
        input_grad,
        inward_grad,
        outward_grad,
        expand_grad,
        shrink_grad,
        gains_grad,
        shifts_grad,
        biases_grad,
        expand_bias_grad,
        inward_new,
        outward_new,
        expand_new,
        shrink_new,
        gains_new,
        shifts_new,
        biases_new,
        expand_bias_new,
        inward_state,
        outward_state,
        expand_state,
        shrink_state,
        gains_state,
        shifts_state,
        biases_state,
        expand_bias_state,
    )


def solution(mesh):
    in_specs = (
        P(("dp", "tensor"), None),
        P(("dp", "tensor"), None),
        P(),
        P("dp", None, "tensor"),
        P("tensor", "dp"),
        P("dp", "tensor"),
        P("tensor", "dp"),
        P(None, ("dp", "tensor")),
        P(None, ("dp", "tensor")),
        P(None, ("dp", "tensor")),
        P(("dp", "tensor")),
        P("dp", None, "tensor"),
        P("tensor", "dp"),
        P("dp", "tensor"),
        P("tensor", "dp"),
        P(None, ("dp", "tensor")),
        P(None, ("dp", "tensor")),
        P(None, ("dp", "tensor")),
        P(("dp", "tensor")),
    )
    out_specs = (
        P(("dp", "tensor"), None),
        P(("dp", "tensor"), None),
        P("dp", None, "tensor"),
        P("tensor", "dp"),
        P("dp", "tensor"),
        P("tensor", "dp"),
        P(None, ("dp", "tensor")),
        P(None, ("dp", "tensor")),
        P(None, ("dp", "tensor")),
        P(("dp", "tensor")),
        P("dp", None, "tensor"),
        P("tensor", "dp"),
        P("dp", "tensor"),
        P("tensor", "dp"),
        P(None, ("dp", "tensor")),
        P(None, ("dp", "tensor")),
        P(None, ("dp", "tensor")),
        P(("dp", "tensor")),
        P("dp", None, "tensor"),
        P("tensor", "dp"),
        P("dp", "tensor"),
        P("tensor", "dp"),
        P(None, ("dp", "tensor")),
        P(None, ("dp", "tensor")),
        P(None, ("dp", "tensor")),
        P(("dp", "tensor")),
    )
    return jax.shard_map(local, mesh=mesh, in_specs=in_specs, out_specs=out_specs, check_vma=False)
```

profile of v0, /device:TPU:0, one launch (start us, length us, event | category | flops | bytes accessed | tf_op | source)
XLA Modules:
  0.0 1968.5 jit_solution(2710539933245299793)
XLA Ops:
  11.3 43.3 %all-gather = f32[32,24,2]{1,2,0:T(2,128)S(1)} all-gather(f32[1,24,2]{1,2,0:T(2,128)S(1)} %bitcast.313), channel_id=1, replica_groups=mesh['dp'=8,'tensor'=4] {'dp','tensor'}, dimensions={0}, use_global_device_ids=true | all-gather | bytes 6336 | tf_op jit(solution)/shard_map/all_gather | solution.py:190
  55.3 36.7 %all-gather.1 = f32[32,24,2]{1,2,0:T(2,128)S(1)} all-gather(f32[1,24,2]{1,2,0:T(2,128)S(1)} %bitcast.312), channel_id=1, replica_groups=mesh['dp'=8,'tensor'=4] {'dp','tensor'}, dimensions={0}, use_global_device_ids=true | all-gather | bytes 6336 | tf_op jit(solution)/shard_map/all_gather | solution.py:191
  93.9 38.5 %all-gather.2 = f32[32,24,4]{1,2,0:T(4,128)S(1)} all-gather(f32[1,24,4]{1,2,0:T(4,128)S(1)} %bitcast.308), channel_id=1, replica_groups=mesh['dp'=8,'tensor'=4] {'dp','tensor'}, dimensions={0}, use_global_device_ids=true | all-gather | bytes 12672 | tf_op jit(solution)/shard_map/all_gather | solution.py:192
  132.5 33.5 %all_gather.51 = bf16[768,3,192]{2,0,1:T(8,128)(2,1)S(1)} all-gather(bf16[96,3,192]{2,0,1:T(8,128)(2,1)S(1)} %convert_element_type.359), channel_id=1, replica_groups=mesh['dp'=8,'tensor'=4] {'dp'}, dimensions={0}, use_global_device_ids=true | all-gather | bytes 995328 | tf_op jit(solution)/shard_map/all_gather | solution.py:196
  180.5 69.1 %all_gather.53 = bf16[192,768]{0,1:T(8,128)(2,1)} all-gather(bf16[192,96]{0,1:T(8,128)(2,1)S(1)} %copy-done.48), channel_id=1, replica_groups=mesh['dp'=8,'tensor'=4] {'dp'}, dimensions={1}, use_global_device_ids=true | all-gather | bytes 331776 | tf_op jit(solution)/shard_map/all_gather | solution.py:197
  265.6 102.8 %while.26 = (s32[]{:T(128)}, bf16[3,512,192]{1,2,0:T(8,128)(2,1)}, f32[3,3,512]{2,1,0:T(4,128)}, s32[3]{0:T(128)}, s32[1536]{0:T(1024)}, /*index=5*/s32[4536]{0:...) while((s32[]{:T(128)}, bf16[3,512,192]{1,2,0:T(8,128)(2,1)}, ...), condition=%wide.region_12.13_spmd, body=%wide.region_5.12_spmd.sunk | while | flops 1424819712 | bytes 157858816 | solution.py:256
  376.5 12.0 all-gather.20.cloned.1.call-start
  388.5 32.9 %reduce-scatter.14.cloned.1.call-done = f32[384,768]{1,0:T(8,128)} async-done(((f32[1536,768]{1,0:T(8,128)}), f32[384,768]{1,0:T(8,128)}) %reduce-scatter.14.cloned.1.call-update) | async-done | bytes 1179664 | tf_op jit(solution)/shard_map/reduce_scatter | solution.py:113
  430.7 40.0 %all-reduce = f32[3072]{0:T(1024)S(1)} all-reduce(f32[3072]{0:T(1024)S(1)} %dynamic-update-slice.6), channel_id=1, replica_groups=mesh['dp'=8,'tensor'=4] {'dp','tensor'}, use_global_device_ids=true, to_apply=%add | all-reduce | flops 3072 | bytes 24576
  478.1 15.9 all-gather.24.cloned.1.call-done
  494.1 23.9 %all-gather.26.cloned.1.call-done = bf16[1536,768]{1,0:T(8,128)(2,1)} async-done(((bf16[384,768]{1,0:T(8,128)(2,1)}), bf16[1536,768]{1,0:T(8,128)(2,1)}) %all-gather.26.cloned.1.call-update) | async-done | bytes 2359312 | tf_op jit(solution)/shard_map/all_gather | solution.py:109
  536.7 41.4 %reduce-scatter.18.cloned.1.call-done = f32[384,768]{1,0:T(8,128)} async-done(((f32[1536,768]{1,0:T(8,128)}), f32[384,768]{1,0:T(8,128)}) %reduce-scatter.18.cloned.1.call-update) | async-done | bytes 1179664 | tf_op jit(solution)/shard_map/reduce_scatter | solution.py:113
  580.9 47.6 %reduce-scatter.16.cloned.1.call-done = f32[384,768]{1,0:T(8,128)} async-done(((f32[1536,768]{1,0:T(8,128)}), f32[384,768]{1,0:T(8,128)}) %reduce-scatter.16.cloned.1.call-update) | async-done | bytes 1179664 | tf_op jit(solution)/shard_map/reduce_scatter | solution.py:113
  640.9 18.3 all-gather.28.cloned.1.call-done
  676.4 280.0 %while.27 = (s32[]{:T(128)}, f32[4536,384]{0,1:T(8,128)}, f32[3,512,192]{1,2,0:T(8,128)}, s32[3]{0:T(128)S(1)}, s32[1536]{0:T(1024)}, /*index=5*/s32[4536]{0:T(1...) while((s32[]{:T(128)}, f32[4536,384]{0,1:T(8,128)}, ...), condition=%wide.region_24.25_spmd, body=%wide.region_20.24_spmd.sunk | while | flops 3498301440 | bytes 327824960 | solution.py:331
  741.8 21.7 %dynamic_update_slice.39 = f32[4536,384]{0,1:T(8,128)} dynamic-update-slice(f32[4536,384]{0,1:T(8,128)} %get-tuple-element.765, f32[3512,384]{0,1:T(8,128)} %dynamic-slice_add_fusion.2, s32[]{:T(128)S(6)} %select_n.125, s32[]{:T(128)} %constant.205.clone.1..sunk.1) | dynamic-update-slice | bytes 10788868 | tf_op jit(solution)/shard_map/while/body/eval_jaxpr/dynamic_update_slice | solution.py:327
  835.4 21.5 %dynamic_update_slice.39 = f32[4536,384]{0,1:T(8,128)} dynamic-update-slice(f32[4536,384]{0,1:T(8,128)} %get-tuple-element.765, f32[3512,384]{0,1:T(8,128)} %dynamic-slice_add_fusion.2, s32[]{:T(128)S(6)} %select_n.125, s32[]{:T(128)} %constant.205.clone.1..sunk.1) | dynamic-update-slice | bytes 10788868 | tf_op jit(solution)/shard_map/while/body/eval_jaxpr/dynamic_update_slice | solution.py:327
  928.3 21.2 %dynamic_update_slice.39 = f32[4536,384]{0,1:T(8,128)} dynamic-update-slice(f32[4536,384]{0,1:T(8,128)} %get-tuple-element.765, f32[3512,384]{0,1:T(8,128)} %dynamic-slice_add_fusion.2, s32[]{:T(128)S(6)} %select_n.125, s32[]{:T(128)} %constant.205.clone.1..sunk.1) | dynamic-update-slice | bytes 10788868 | tf_op jit(solution)/shard_map/while/body/eval_jaxpr/dynamic_update_slice | solution.py:327
  976.7 38.7 %collective-permute-done.2 = bf16[1500,384]{1,0:T(8,128)(2,1)} collective-permute-done((bf16[1500,384]{1,0:T(8,128)(2,1)}, bf16[1500,384]{1,0:T(8,128)(2,1)}, u32[]{:S(2)}, u32[]{:S(2)}) %collective-permute-start.2) | collective-permute-done | bytes 1152032 | tf_op jit(solution)/shard_map/ppermute | solution.py:34
  1020.4 8.7 concatenate.33
  1039.3 9.2 scatter-add.6
  1052.9 10.5 scatter-add.9
  1079.2 88.5 %reduce-scatter.22.cloned.1.call-done = f32[96,3,192]{2,0,1:T(8,128)} async-done(((f32[768,3,192]{2,0,1:T(8,128)}), f32[96,3,192]{2,0,1:T(8,128)}) %reduce-scatter.22.cloned.1.call-update) | async-done | bytes 221200 | tf_op jit(solution)/shard_map/reduce_scatter | solution.py:355
  1175.3 49.0 %all-gather.34.cloned.1.call-done = bf16[32,1,18432]{2,1,0:T(2,128)(2,1)} async-done(((bf16[1,1,18432]{2,1,0:T(2,128)(2,1)}), bf16[32,1,18432]{2,1,0:T(2,128)(2,1)}) %all-gather.34.cloned.1.call-update) | async-done | bytes 1179664 | tf_op jit(solution)/shard_map/all_gather | solution.py:407
  1224.3 13.6 conditional.3
  1244.1 63.9 %all-gather.32.cloned.1.call-done = bf16[32,1,73728]{2,1,0:T(2,128)(2,1)} async-done(((bf16[1,1,73728]{2,1,0:T(2,128)(2,1)}), bf16[32,1,73728]{2,1,0:T(2,128)(2,1)}) %all-gather.32.cloned.1.call-update) | async-done | bytes 4718608 | tf_op jit(solution)/shard_map/all_gather | solution.py:409
  1308.0 74.0 %all-gather.30.cloned.1.call-done = bf16[32,1,55296]{2,1,0:T(2,128)(2,1)} async-done(((bf16[1,1,55296]{2,1,0:T(2,128)(2,1)}), bf16[32,1,55296]{2,1,0:T(2,128)(2,1)}) %all-gather.30.cloned.1.call-update) | async-done | bytes 3538960 | tf_op jit(solution)/shard_map/all_gather | solution.py:406
  1382.0 314.7 %conditional.2 = (bf16[32,55296]{1,0:T(8,128)(2,1)}, bf16[32,73728]{1,0:T(8,128)(2,1)}) conditional(s32[]{:T(128)} %convert_element_type.375, () %tuple.42, (bf16[32,1,55296]{2,1,0:T(2,128)(2,1)}, bf16[32,1,73728]{2,1,0:T(2,128)(2,1)}) %tuple.43), branch_computations={%region_45.46_spmd, %region_46.49_spmd} | conditional | flops 43582095360 | bytes 280756352 | solution.py:448
  1382.0 29.1 %reduce.6 = bf16[32,73728]{1,0:T(8,128)(2,1)} reduce(bf16[32,1,73728]{2,1,0:T(2,128)(2,1)} %get-tuple-element.420, bf16[]{:T(256)} %constant.256), dimensions={1}, to_apply=%get-tuple-element.420.reduce_sub_computation | reduce | bytes 9437186 | tf_op jit(solution)/shard_map/cond
  1411.1 8.8 reshape.356
  1419.9 10.1 copy.191
  1449.0 10.3 add_convert_fusion.2
  1466.9 10.1 add_convert_fusion.1
  1484.6 10.1 fusion.56
  1494.7 9.7 reshape.358
  1504.4 10.1 copy.192
  1514.5 11.9 reshape.359
  1526.4 74.7 %reduce.5 = bf16[32,55296]{1,0:T(8,128)(2,1)S(1)} reduce(bf16[32,1,55296]{2,1,0:T(2,128)(2,1)} %get-tuple-element.419, bf16[]{:T(256)} %constant.256), dimensions={1}, to_apply=%get-tuple-element.419.reduce_sub_computation | reduce | bytes 7077890 | tf_op jit(solution)/shard_map/cond
  1601.2 8.3 reshape.352
  1609.5 11.0 copy.189
  1620.4 7.8 reshape.353
  1637.8 8.2 add_convert_fusion.5
  1650.0 8.1 add_convert_fusion.4
  1665.3 8.2 add_convert_fusion.3
  1679.3 8.3 copy.245
  1687.6 8.9 reshape.355
  1723.7 39.6 %all-reduce.5 = (f32[2,768]{1,0:T(2,128)}, f32[2,768]{1,0:T(2,128)}, f32[4,768]{1,0:T(4,128)}, f32[3072]{0:T(1024)}) all-reduce(f32[2,768]{1,0:T(2,128)} %pad_maximum_fusion.2, f32[2,768]{1,0:T(2,128)} %pad_maximum_fusion.3, f32[4,768]{1,0:T(4,128)} %pad_maximum_fusion.1, ...), channel_id=10, replica_groups=mesh['dp'=8,'tensor'=4] {'dp','tensor'}, use_global_device_ids=true, to_apply=%region_34.35.clone | all-reduce | flops 9216 | bytes 73728
  1771.5 176.6 %all-reduce.9.cloned.1.call-done = (bf16[32,129024]{1,0:T(8,128)(2,1)}, bf16[32,92160]{1,0:T(8,128)(2,1)}) async-done(((bf16[32,129024]{1,0:T(8,128)(2,1)}, bf16[32,92160]{1,0:T(8,128)(2,1)}), (bf16[32,129024]{1,0:T(8,128)(2,1)}, bf16[32,92160]{1,0:T(8,128)(2,1)})) %all-reduce.9.cloned.1.call-update) | async-done | bytes 14155792 | tf_op jit(solution)/shard_map/psum | solution.py:45
  (646 shorter events, 604.1 us)
Async XLA Ops:
  8.0 84.7 %copy-start.12 = (f32[384,768]{1,0:T(8,128)S(1)}, f32[384,768]{1,0:T(8,128)}, u32[]{:S(2)}) copy-start(f32[384,768]{1,0:T(8,128)} %param.31) | copy-start | bytes 3538948
  8.1 47.3 %copy-start.70 = (f32[2,24]{1,0:T(2,128)S(1)}, f32[2,24]{1,0:T(2,128)}, u32[]{:S(2)}) copy-start(f32[2,24]{1,0:T(2,128)} %param.39) | copy-start | bytes 580
  8.1 85.9 %copy-start.69 = (f32[4,24]{1,0:T(4,128)S(1)}, f32[4,24]{1,0:T(4,128)}, u32[]{:S(2)}) copy-start(f32[4,24]{1,0:T(4,128)} %param.40) | copy-start | bytes 1156
  8.1 160.9 %all-gather.18.cloned.1.call-start = ((), (), s32[]{:S(2)}) async-start(), calls=%async_computation.8 | async-start | bytes 2949120 | tf_op jit(solution)/shard_map/all_gather | solution.py:109
  9.6 122.9 %copy-start.36 = (f32[96,3,192]{2,0,1:T(8,128)S(1)}, f32[96,3,192]{2,0,1:T(8,128)}, u32[]{:S(2)}) copy-start(f32[96,3,192]{2,0,1:T(8,128)} %param.34) | copy-start | bytes 663556
  9.6 84.3 %copy-start.54 = (f32[384]{0:T(512)}, f32[384]{0:T(512)S(1)}, u32[]{:S(2)}) copy-start(f32[384]{0:T(512)S(1)} %broadcast_multiply_fusion.5) | copy-start | bytes 4612
  11.2 82.7 %copy-start.61 = (f32[384]{0:T(512)}, f32[384]{0:T(512)S(1)}, u32[]{:S(2)}) copy-start(f32[384]{0:T(512)S(1)} %add_rsqrt_fusion.1) | copy-start | bytes 4612
  55.3 38.6 %copy-start.52 = (f32[768]{0:T(1024)}, f32[768]{0:T(1024)S(1)}, u32[]{:S(2)}) copy-start(f32[768]{0:T(1024)S(1)} %get-tuple-element.437) | copy-start | bytes 9220
  93.8 72.9 %copy-start.74 = (s32[12]{0:T(128)S(1)}, s32[12]{0:T(128)}, u32[]{:S(2)}) copy-start(s32[12]{0:T(128)} %param.33) | copy-start | bytes 148
  93.8 73.1 %copy-start.44 = (f32[192,96]{1,0:T(8,128)S(1)}, f32[192,96]{1,0:T(8,128)}, u32[]{:S(2)}) copy-start(f32[192,96]{1,0:T(8,128)} %param.35) | copy-start | bytes 221188
  93.8 327.6 %reduce-scatter.14.cloned.1.call-start = ((), (), s32[]{:S(2)}) async-start(), calls=%async_computation.9 | async-start | bytes 5898240 | tf_op jit(solution)/shard_map/reduce_scatter | solution.py:113
  175.1 75.8 %copy-start.31 = (bf16[1536,192]{0,1:T(8,128)(2,1)S(1)}, bf16[1536,192]{0,1:T(8,128)(2,1)}, u32[]{:S(2)}) copy-start(bf16[1536,192]{0,1:T(8,128)(2,1)} %get-tuple-element.523) | copy-start | bytes 1769476
  175.1 77.0 %collective-permute-start = (bf16[1500,384]{1,0:T(8,128)(2,1)}, bf16[1500,384]{1,0:T(8,128)(2,1)}, u32[]{:S(2)}, u32[]{:S(2)}) collective-permute-start(bf16[1500,384]{1,0:T(8,128)(2,1)} %copy.201), channel_id=1, source_target_pairs={{0,4},{4,8},{8,12},{12,16},{16,20},{20,24},{24,28},{1,5},{5,9},{9,... | collective-permute-start | bytes 3456008 | tf_op jit(solution)/shard_map/ppermute | solution.py:34
  179.0 74.8 %collective-permute-start.1 = (bf16[1500,384]{1,0:T(8,128)(2,1)}, bf16[1500,384]{1,0:T(8,128)(2,1)}, u32[]{:S(2)}, u32[]{:S(2)}) collective-permute-start(bf16[1500,384]{1,0:T(8,128)(2,1)} %copy.202), channel_id=1, source_target_pairs={{4,0},{8,4},{12,8},{16,12},{20,16},{24,20},{28,24},{5,1},{9,5},{13... | collective-permute-start | bytes 3456008 | tf_op jit(solution)/shard_map/ppermute | solution.py:36
  374.7 46.7 %copy-start.66 = (f32[768]{0:T(1024)S(1)}, f32[768]{0:T(1024)}, u32[]{:S(2)}) copy-start(f32[768]{0:T(1024)} %get-tuple-element.435) | copy-start | bytes 9220
  374.8 96.0 %all-gather.22.cloned.1.call-start = ((), (), s32[]{:S(2)}) async-start(), calls=%async_computation.11 | async-start | bytes 1327104 | tf_op jit(solution)/shard_map/all_gather | solution.py:198
  376.5 94.3 %all-gather.20.cloned.1.call-start = ((), (), s32[]{:S(2)}) async-start(), calls=%async_computation.10 | async-start | bytes 2949120 | tf_op jit(solution)/shard_map/all_gather | solution.py:109
  425.4 68.7 %all-gather.24.cloned.1.call-start = ((), (), s32[]{:S(2)}) async-start(), calls=%async_computation.12 | async-start | bytes 1327104 | tf_op jit(solution)/shard_map/all_gather | solution.py:199
  427.1 90.9 %all-gather.26.cloned.1.call-start = ((), (), s32[]{:S(2)}) async-start(), calls=%async_computation.14 | async-start | bytes 2949120 | tf_op jit(solution)/shard_map/all_gather | solution.py:109
  430.3 147.8 %reduce-scatter.18.cloned.1.call-start = ((), (), s32[]{:S(2)}) async-start(), calls=%async_computation.15 | async-start | bytes 5898240 | tf_op jit(solution)/shard_map/reduce_scatter | solution.py:113
  530.2 98.3 %reduce-scatter.16.cloned.1.call-start = ((), (), s32[]{:S(2)}) async-start(), calls=%async_computation.13 | async-start | bytes 5898240 | tf_op jit(solution)/shard_map/reduce_scatter | solution.py:113
  536.7 91.9 %copy-start.65 = (f32[768]{0:T(1024)S(1)}, f32[768]{0:T(1024)}, u32[]{:S(2)}) copy-start(f32[768]{0:T(1024)} %get-tuple-element.434) | copy-start | bytes 9220
  536.7 122.4 %all-gather.28.cloned.1.call-start = ((), (), s32[]{:S(2)}) async-start(), calls=%async_computation.16 | async-start | bytes 2949120 | tf_op jit(solution)/shard_map/all_gather | solution.py:109
  634.9 435.2 %reduce-scatter.24.cloned.1.call-start = ((), (), s32[]{:S(2)}) async-start(), calls=%async_computation.19 | async-start | bytes 2654208 | tf_op jit(solution)/shard_map/reduce_scatter | solution.py:357
  640.8 432.8 %reduce-scatter.28.cloned.1.call-start = ((), (), s32[]{:S(2)}) async-start(), calls=%async_computation.25 | async-start | bytes 884736
  663.0 413.1 %reduce-scatter.26.cloned.1.call-start = ((), (), s32[]{:S(2)}) async-start(), calls=%async_computation.20 | async-start | bytes 2654208 | tf_op jit(solution)/shard_map/reduce_scatter | solution.py:358
  669.1 498.7 %reduce-scatter.22.cloned.1.call-start = ((), (), s32[]{:S(2)}) async-start(), calls=%async_computation.18 | async-start | bytes 2654208 | tf_op jit(solution)/shard_map/reduce_scatter | solution.py:355
  676.8 30.6 %copy-start.6 = (bf16[4536,384]{1,0:T(8,128)(2,1)}, bf16[4536,384]{1,0:T(8,128)(2,1)S(1)}, u32[]{:S(2)}) copy-start(bf16[4536,384]{1,0:T(8,128)(2,1)S(1)} %get-tuple-element.794) | copy-start | bytes 10450948 | tf_op jit(solution)/shard_map/while
  741.7 21.8 %copy-start.7 = (bf16[4536,384]{1,0:T(8,128)(2,1)S(1)}, bf16[4536,384]{1,0:T(8,128)(2,1)}, u32[]{:S(2)}) copy-start(bf16[4536,384]{1,0:T(8,128)(2,1)} %copy-done.6) | copy-start | bytes 10450948 | tf_op jit(solution)/shard_map/while
  770.3 30.4 %copy-start.6 = (bf16[4536,384]{1,0:T(8,128)(2,1)}, bf16[4536,384]{1,0:T(8,128)(2,1)S(1)}, u32[]{:S(2)}) copy-start(bf16[4536,384]{1,0:T(8,128)(2,1)S(1)} %get-tuple-element.794) | copy-start | bytes 10450948 | tf_op jit(solution)/shard_map/while
  835.4 21.5 %copy-start.7 = (bf16[4536,384]{1,0:T(8,128)(2,1)S(1)}, bf16[4536,384]{1,0:T(8,128)(2,1)}, u32[]{:S(2)}) copy-start(bf16[4536,384]{1,0:T(8,128)(2,1)} %copy-done.6) | copy-start | bytes 10450948 | tf_op jit(solution)/shard_map/while
  863.7 30.3 %copy-start.6 = (bf16[4536,384]{1,0:T(8,128)(2,1)}, bf16[4536,384]{1,0:T(8,128)(2,1)S(1)}, u32[]{:S(2)}) copy-start(bf16[4536,384]{1,0:T(8,128)(2,1)S(1)} %get-tuple-element.794) | copy-start | bytes 10450948 | tf_op jit(solution)/shard_map/while
  928.3 21.2 %copy-start.7 = (bf16[4536,384]{1,0:T(8,128)(2,1)S(1)}, bf16[4536,384]{1,0:T(8,128)(2,1)}, u32[]{:S(2)}) copy-start(bf16[4536,384]{1,0:T(8,128)(2,1)} %copy-done.6) | copy-start | bytes 10450948 | tf_op jit(solution)/shard_map/while
  961.7 53.7 %collective-permute-start.2 = (bf16[1500,384]{1,0:T(8,128)(2,1)}, bf16[1500,384]{1,0:T(8,128)(2,1)}, u32[]{:S(2)}, u32[]{:S(2)}) collective-permute-start(bf16[1500,384]{1,0:T(8,128)(2,1)} %copy.213), channel_id=1, source_target_pairs={{0,4},{4,8},{8,12},{12,16},{16,20},{20,24},{24,28},{1,5},{5,9},{9,... | collective-permute-start | bytes 3456008 | tf_op jit(solution)/shard_map/ppermute | solution.py:34
  967.6 50.4 %collective-permute-start.3 = (bf16[1500,384]{1,0:T(8,128)(2,1)}, bf16[1500,384]{1,0:T(8,128)(2,1)}, u32[]{:S(2)}, u32[]{:S(2)}) collective-permute-start(bf16[1500,384]{1,0:T(8,128)(2,1)} %copy.214), channel_id=1, source_target_pairs={{4,0},{8,4},{12,8},{16,12},{20,16},{24,20},{28,24},{5,1},{9,5},{13... | collective-permute-start | bytes 3456008 | tf_op jit(solution)/shard_map/ppermute | solution.py:36
  1070.1 105.2 %all-gather.36.cloned.1.call-start = ((), (), s32[]{:S(2)}) async-start(), calls=%async_computation.24 | async-start | bytes 9732096 | tf_op jit(solution)/shard_map/all_gather | solution.py:408
  1073.5 150.8 %all-gather.34.cloned.1.call-start = ((), (), s32[]{:S(2)}) async-start(), calls=%async_computation.23 | async-start | bytes 2433024 | tf_op jit(solution)/shard_map/all_gather | solution.py:407
  1074.6 96.3 %copy-start.27 = (bf16[768,3,192]{2,0,1:T(8,128)(2,1)S(1)}, bf16[768,3,192]{2,0,1:T(8,128)(2,1)}, u32[]{:S(2)}) copy-start(bf16[768,3,192]{2,0,1:T(8,128)(2,1)} %copy-done.26) | copy-start | bytes 2654212
  1074.6 96.3 %copy-start.40 = (bf16[1536,1,192]{0,2,1:T(8,128)(2,1)S(1)}, bf16[1536,1,192]{0,2,1:T(8,128)(2,1)}, u32[]{:S(2)}) copy-start(bf16[1536,1,192]{0,2,1:T(8,128)(2,1)} %copy-done.39) | copy-start | bytes 1769476
  1076.1 231.9 %all-gather.32.cloned.1.call-start = ((), (), s32[]{:S(2)}) async-start(), calls=%async_computation.22 | async-start | bytes 9732096 | tf_op jit(solution)/shard_map/all_gather | solution.py:409
  1079.2 302.8 %all-gather.30.cloned.1.call-start = ((), (), s32[]{:S(2)}) async-start(), calls=%async_computation.21 | async-start | bytes 7299072 | tf_op jit(solution)/shard_map/all_gather | solution.py:406
  1170.6 548.6 %reduce-scatter.20.cloned.1.call-start = ((), (), s32[]{:S(2)}) async-start(), calls=%async_computation.17 | async-start | bytes 5898240 | tf_op jit(solution)/shard_map/reduce_scatter | solution.py:113
  1175.2 772.8 %all-reduce.9.cloned.1.call-start = ((), (), s32[]{:S(2)}) async-start(), calls=%async_computation.26 | async-start | bytes 28311552 | tf_op jit(solution)/shard_map/psum | solution.py:45
  1704.0 15.3 copy-start.13
  1704.0 15.3 copy-start.53
  1717.1 53.0 %copy-start.22 = (f32[384,768]{1,0:T(8,128)S(1)}, f32[384,768]{1,0:T(8,128)}, u32[]{:S(2)}) copy-start(f32[384,768]{1,0:T(8,128)} %copy-done.21) | copy-start | bytes 3538948
  1719.3 50.8 %copy-start.28 = (f32[384,768]{1,0:T(8,128)S(1)}, f32[384,768]{1,0:T(8,128)}, u32[]{:S(2)}) copy-start(f32[384,768]{1,0:T(8,128)} %reduce-scatter.20.cloned.1.call-done) | copy-start | bytes 3538948
  1771.5 183.2 %copy-start.37 = (f32[96,3,192]{2,0,1:T(8,128)S(1)}, f32[96,3,192]{2,0,1:T(8,128)}, u32[]{:S(2)}) copy-start(f32[96,3,192]{2,0,1:T(8,128)} %param.34) | copy-start | bytes 663556
  (126 other events, 589.4 us)
Sparse Core Ops, SparseCore 0:
  93.9 21.7 all-gather.17
  374.9 46.4 reduce-scatter.13
  635.0 24.0 all-gather.27
  1074.1 90.4 all-gather.35
  1167.8 56.3 all-gather.33
  1227.6 80.3 all-gather.31
  1311.5 70.4 all-gather.29
  1384.5 46.5 reduce-scatter.19
  1704.1 243.8 all-reduce.8
Sparse Core Ops, SparseCore 1:
  378.0 39.9 all-gather.21
  425.5 24.6 all-gather.19
  452.7 41.3 all-gather.23
  495.7 22.2 all-gather.25
  530.3 47.8 reduce-scatter.17
  580.7 47.8 reduce-scatter.15
  640.9 70.0 reduce-scatter.23
  714.2 62.4 reduce-scatter.27
  780.6 68.8 reduce-scatter.25
  1070.2 97.5 reduce-scatter.21
where the time goes:
time: 1980 us; the launch traced here: 1970 us
  waiting for transfers between devices  671 us (34%)
  matrix products  364 us (18%)
  local copies, waits for them, and re-layouts  334 us (17%)
  blocking collectives  301 us (15%)
  other arithmetic  241 us (12%)
  starting transfers between devices  22.4 us (1%)
    psum x1, waiting for transfers between devices, from_root(): return lax.psum(kept, axis)  177 us
    dot_general x31, matrix products, contract_last(): lax.dot_general(left, right, (((1,), (1,)), ((), ())), preferred_element_...  125 us
    reduce_scatter x4, waiting for transfers between devices, sum_rows(): lax.psum_scatter(producer(jnp.int32(0), count * lax.axis_size('tensor')),...  122 us
    cond x2, other arithmetic  104 us
    reduce_scatter x1, waiting for transfers between devices, local(): lax.psum_scatter(inward_part, 'dp', scatter_dimension=0, tiled=True)  88.5 us
    unnamed x2, blocking collectives  79.6 us
    all_gather x1, waiting for transfers between devices, local(): lax.all_gather(flat_in, ('dp', 'tensor'), axis=0, tiled=True)  74 us
    all_gather x1, blocking collectives, local(): lax.all_gather(outward_weight.astype(jnp.bfloat16), 'dp', axis=1, tiled=T...  69.1 us
  transfers between devices with their start and end apart: 23, of which 12 were waited for; matrix products, arithmetic and copies ran while one was open for 39% of the time, Pallas kernels for 0%

commit v1 on v0

v1 whole, which is shorter than its diff:
```python
import functools
import math

import jax
import jax.numpy as jnp
from jax import lax
from jax.experimental import pallas as pl
from jax.experimental.pallas import tpu as pltpu
from jax.sharding import PartitionSpec as P

HDIM = 64
MAXCLIP = 1500
NS_STEPS = 3
LANES = 128
NEG = -1e30

norm_epsilon = 1e-05
frobenius_epsilon = 1e-07
quintic_one = 3.4445
quintic_two = -4.775
quintic_three = 2.0315
momentum_decay = 0.9
learn_rate = 0.2
vector_rate = 0.003
root_half = 0.7071067811865476
gauss_factor = 0.3989422804014327


def over_last(left, right):
    return lax.dot_general(left, right, (((1,), (1,)), ((), ())), preferred_element_type=jnp.float32)


def over_first(left, right):
    return lax.dot_general(left, right, (((0,), (0,)), ((), ())), preferred_element_type=jnp.float32)


def picker(shape, heads, head, inner, flip):
    packed = lax.broadcasted_iota(jnp.int32, shape, 0 if not flip else 1)
    slot = lax.broadcasted_iota(jnp.int32, shape, 1 if not flip else 0)
    hit = (packed - head * HDIM == slot - inner) & (slot >= inner) & (slot < inner + HDIM)
    return jnp.where(hit, 1.0, 0.0).astype(jnp.bfloat16)


def clip_rows(clips_ref, count, cols, first):
    pos = first + lax.broadcasted_iota(jnp.int32, (1, cols), 1)

    def step(i, carry):
        end, start_row, end_row = carry
        stop = end + clips_ref[i]
        inside = (pos >= end) & (pos < stop)
        return stop, jnp.where(inside, end, start_row), jnp.where(inside, stop, end_row)

    zero = jnp.zeros((1, cols), jnp.int32)
    return lax.fori_loop(0, count, step, (jnp.int32(0), zero, zero))[1:]


def clip_span(clips_ref, count, first, last):
    def step(i, carry):
        end, low, high = carry
        stop = end + clips_ref[i]
        low = jnp.where((first >= end) & (first < stop), end, low)
        high = jnp.where((last >= end) & (last < stop), stop, high)
        return stop, low, high

    return lax.fori_loop(0, count, step, (jnp.int32(0), jnp.int32(0), jnp.int32(0)))[1:]


def block_bias(start_row, end_row, key_first, bk, bq):
    key = key_first + lax.broadcasted_iota(jnp.int32, (bk, bq), 0)
    return jnp.where((key >= start_row) & (key < end_row), 0.0, NEG)


def forward_body(heads, bq, bk, count, clips_ref, base_ref, q_ref, kv_ref, o_ref, lse_ref):
    run = q_ref.shape[0]
    base = base_ref[0]
    ext = base - run

    @pl.loop(0, run // bq)
    def _(i):
        first = base + i * bq
        rows = pl.ds(pl.multiple_of(i * bq, bq), bq)
        start_row, end_row = clip_rows(clips_ref, count, bq, first)
        low, high = clip_span(clips_ref, count, first, first + bq - 1)
        lo = (low - ext) // bk
        hi = (high - ext + bk - 1) // bk

        def step(j, carry):
            bias = block_bias(start_row, end_row, ext + j * bk, bk, bq)
            keys = pl.ds(pl.multiple_of(j * bk, bk), bk)
            out = []
            for head in range(heads):
                m, l, acc = carry[head]
                cols = slice(head * LANES, (head + 1) * LANES)
                kv = kv_ref[keys, cols]
                s = over_last(kv, q_ref[rows, cols]) + bias
                m_new = jnp.maximum(m, jnp.max(s, axis=0, keepdims=True))
                p = jnp.exp(s - m_new)
                alpha = jnp.exp(m - m_new)
                l = l * alpha + jnp.sum(p, axis=0, keepdims=True)
                acc = acc * alpha + over_first(kv, p.astype(jnp.bfloat16))
                out.append((m_new, l, acc))
            return tuple(out)

        init = tuple(
            (jnp.full((1, bq), NEG, jnp.float32), jnp.zeros((1, bq), jnp.float32), jnp.zeros((LANES, bq), jnp.float32))
            for _ in range(heads)
        )
        final = lax.fori_loop(lo, hi, step, init)
        total = None
        lse = []
        for head in range(heads):
            m, l, acc = final[head]
            o = (acc / l).astype(jnp.bfloat16)
            part = over_first(o, picker((LANES, heads * HDIM), heads, head, HDIM, True))
            total = part if total is None else total + part
            lse.append(m + jnp.log(l))
        lse.append(jnp.zeros((8 - heads, bq), jnp.float32))
        o_ref[rows, :] = total.astype(jnp.bfloat16)
        lse_ref[:, rows] = jnp.concatenate(lse, axis=0)


def backward_body(heads, bq, bk, count, clips_ref, base_ref, q_ref, kv_ref, o_ref, do_ref, lse_ref,
                  dq_ref, own_ref, rim_ref, sums_ref, dkv_ref, doz_ref):
    run = q_ref.shape[0]
    base = base_ref[0]
    ext = base - run
    scale = 1.0 / math.sqrt(HDIM)
    width = heads * HDIM
    dkv_ref[...] = jnp.zeros_like(dkv_ref)

    @pl.loop(0, run // bq)
    def _(i):
        first = base + i * bq
        rows = pl.ds(pl.multiple_of(i * bq, bq), bq)
        start_row, end_row = clip_rows(clips_ref, count, bq, first)
        low, high = clip_span(clips_ref, count, first, first + bq - 1)
        lo = (low - ext) // bk
        hi = (high - ext + bk - 1) // bk
        do = do_ref[rows, :]
        prod = do.astype(jnp.float32) * o_ref[rows, :].astype(jnp.float32)
        prod_hi = prod.astype(jnp.bfloat16)
        prod_lo = (prod - prod_hi.astype(jnp.float32)).astype(jnp.bfloat16)
        sel_row = lax.broadcasted_iota(jnp.int32, (8, width), 0)
        sel_col = lax.broadcasted_iota(jnp.int32, (8, width), 1)
        sel = jnp.where((sel_col >= sel_row * HDIM) & (sel_col < (sel_row + 1) * HDIM), 1.0, 0.0).astype(jnp.bfloat16)
        delta = over_last(sel, prod_hi) + over_last(sel, prod_lo)
        lse = lse_ref[:, rows]
        for head in range(heads):
            doz_ref[:, head * LANES:(head + 1) * LANES] = jnp.dot(
                do, picker((width, LANES), heads, head, HDIM, False), preferred_element_type=jnp.float32
            ).astype(jnp.bfloat16)

        def step(j, carry):
            bias = block_bias(start_row, end_row, ext + j * bk, bk, bq)
            keys = pl.ds(pl.multiple_of(j * bk, bk), bk)
            out = []
            for head in range(heads):
                cols = slice(head * LANES, (head + 1) * LANES)
                kv = kv_ref[keys, cols]
                qs = q_ref[rows, cols]
                doz = doz_ref[:, cols]
                p = jnp.exp(over_last(kv, qs) + bias - lse[head:head + 1])
                ds = (p * (over_last(kv, doz) - delta[head:head + 1])).astype(jnp.bfloat16)
                dkv_ref[keys, cols] += jnp.dot(ds, qs, preferred_element_type=jnp.float32) + jnp.dot(
                    p.astype(jnp.bfloat16), doz, preferred_element_type=jnp.float32)
                out.append(carry[head] + over_first(kv, ds))
            return tuple(out)

        init = tuple(jnp.zeros((LANES, bq), jnp.float32) for _ in range(heads))
        final = lax.fori_loop(lo, hi, step, init)
        for head in range(heads):
            dq_ref[rows, head * LANES:(head + 1) * LANES] = (final[head] * scale).T.astype(jnp.bfloat16)
    own_ref[...] = dkv_ref[pl.ds(run, run), :]
    rim_ref[0] = dkv_ref[pl.ds(0, run), :].astype(jnp.bfloat16)
    rim_ref[1] = dkv_ref[pl.ds(2 * run, run), :].astype(jnp.bfloat16)
    sums_ref[...] = jnp.zeros_like(sums_ref)


VM = pl.BlockSpec(memory_space=pltpu.VMEM)
SM = pl.BlockSpec(memory_space=pltpu.SMEM)


def attend_forward(clips, base, q, kv, heads, bq, bk):
    run = q.shape[0]
    return pl.pallas_call(
        functools.partial(forward_body, heads, bq, bk, clips.shape[0]),
        out_shape=(jax.ShapeDtypeStruct((run, heads * HDIM), jnp.bfloat16), jax.ShapeDtypeStruct((8, run), jnp.float32)),
        in_specs=[SM, SM, VM, VM],
        out_specs=(VM, VM),
        name="attend_forward",
    )(clips, base, q, kv)


def attend_backward(clips, base, q, kv, o, do, lse, heads, bq, bk):
    run = q.shape[0]
    wide = heads * LANES
    return pl.pallas_call(
        functools.partial(backward_body, heads, bq, bk, clips.shape[0]),
        out_shape=(
            jax.ShapeDtypeStruct((run, wide), jnp.bfloat16),
            jax.ShapeDtypeStruct((run, wide), jnp.float32),
            jax.ShapeDtypeStruct((2, run, wide), jnp.bfloat16),
            jax.ShapeDtypeStruct((8, wide), jnp.float32),
        ),
        in_specs=[SM, SM, VM, VM, VM, VM, VM],
        out_specs=(VM, VM, VM, VM),
        scratch_shapes=[pltpu.VMEM((3 * run, wide), jnp.float32), pltpu.VMEM((bq, wide), jnp.bfloat16)],
        name="attend_backward",
    )(clips, base, q, kv, o, do, lse)


class Seat:
    def __init__(self, data_count):
        self.planes = data_count // 2
        self.d = lax.axis_index("dp")
        self.t = lax.axis_index("tensor")
        self.h, self.l = self.d // 2, self.d % 2
        self.x, self.c = self.t // 2, self.t % 2
        self.run = 2 * self.h + self.c
        self.spot = 4 * self.l + self.t


def at(h, l, x, c):
    return {"dp": 2 * h + l, "tensor": 2 * x + c}


def flip(value, by):
    return (value + by) % 2


def shift(h, by, planes):
    return (h + by) % planes


class Mail:
    def __init__(self, send, recv):
        self.send_sems, self.recv_sems = send, recv
        self.sent = 0
        self.todo = []

    def copy(self, src, dst, target, slot):
        return pltpu.make_async_remote_copy(
            src_ref=src, dst_ref=dst, send_sem=self.send_sems.at[self.sent], recv_sem=self.recv_sems.at[slot],
            device_id=target, device_id_type=pl.DeviceIdType.MESH,
        )

    def post(self, src, dst, target, slot, keep=None, local=None):
        copy = self.copy(src, dst, target, slot)
        self.sent += 1
        if keep is None:
            copy.start()
        else:
            pl.when(jnp.logical_not(keep))(copy.start)
            if local is not None:
                pl.when(keep)(local)
        self.todo.append((copy, keep))

    def drain(self):
        for copy, keep in self.todo:
            if keep is None:
                copy.wait_send()
            else:
                pl.when(jnp.logical_not(keep))(copy.wait_send)
        self.todo = []

    def take(self, dst, target, slot, keep=None):
        copy = pltpu.make_async_remote_copy(
            src_ref=dst, dst_ref=dst, send_sem=self.send_sems.at[0], recv_sem=self.recv_sems.at[slot],
            device_id=target, device_id_type=pl.DeviceIdType.MESH,
        )
        if keep is None:
            copy.wait_recv()
        else:
            pl.when(jnp.logical_not(keep))(copy.wait_recv)


def greet(peers):
    barrier = pltpu.get_barrier_semaphore()
    for peer in peers:
        pl.semaphore_signal(barrier, inc=1, device_id=peer, device_id_type=pl.DeviceIdType.MESH)
    pl.semaphore_wait(barrier, len(peers))


def plane_peers(me):
    return [
        at(me.h, flip(me.l, fl), flip(me.x, fx), flip(me.c, fc))
        for fl in (0, 1) for fx in (0, 1) for fc in (0, 1) if fl + fx + fc
    ]


def column_peers(me):
    return [
        at(shift(me.h, dh, me.planes), flip(me.l, fl), me.x, flip(me.c, fc))
        for dh in range(1, me.planes) for fl in (0, 1) for fc in (0, 1)
    ]


def line_peers(me):
    return [
        at(shift(me.h, dh, me.planes), flip(me.l, fl), me.x, me.c)
        for dh in range(me.planes) for fl in (0, 1) if dh + fl
    ]


def sibling(me):
    return at(me.h, me.l, me.x, flip(me.c, 1))


def call(body, name, number, data_count, arrays, outs, sends, recvs, limit=None):
    def kernel(*refs):
        count = len(arrays)
        ins, rest = refs[:count], refs[count:]
        body(Seat(data_count), Mail(rest[-2], rest[-1]), ins, rest[:len(outs)])

    return pl.pallas_call(
        kernel,
        out_shape=tuple(jax.ShapeDtypeStruct(*o) for o in outs),
        in_specs=[pl.BlockSpec(memory_space=pltpu.VMEM)] * len(arrays),
        out_specs=(pl.BlockSpec(memory_space=pltpu.VMEM),) * len(outs),
        scratch_shapes=[pltpu.SemaphoreType.DMA((sends,)), pltpu.SemaphoreType.DMA((recvs,))],
        compiler_params=pltpu.CompilerParams(collective_id=number, has_side_effects=True),
        name=name,
    )(*arrays)


def begin_body(me, mail, ins, outs):
    vec, win, rows_in, cot_in = ins
    vec_all, weights, chip_in, chip_cot = outs
    planes = me.planes
    greet(plane_peers(me) + column_peers(me))
    vec_slot = lambda i: i
    z_slot = lambda i: 8 + i
    w_slot = lambda i: 8 + planes + i
    r_slot = 8 + 3 * planes
    for fl in (0, 1):
        for fx in (0, 1):
            for fc in (0, 1):
                if fl + fx + fc:
                    mail.post(vec, vec_all.at[me.h, me.spot], at(me.h, flip(me.l, fl), flip(me.x, fx), flip(me.c, fc)), vec_slot(me.spot))
    vec_all[me.h, me.spot] = vec[...]
    mine = me.l == me.c

    def keep_weights():
        weights[me.d] = win[...]

    for dh in range(planes):
        for fc in (0, 1):
            local = dh + fc == 0
            mail.post(win, weights.at[me.d], at(shift(me.h, dh, planes), me.c, me.x, flip(me.c, fc)), w_slot(me.d),
                      mine if local else None, keep_weights if local else None)
    mail.post(rows_in, chip_in.at[me.c], sibling(me), r_slot)
    mail.post(cot_in, chip_cot.at[me.c], sibling(me), r_slot + 1)
    chip_in[me.c] = rows_in[...]
    chip_cot[me.c] = cot_in[...]
    for fl in (0, 1):
        for fx in (0, 1):
            for fc in (0, 1):
                if fl + fx + fc:
                    l, x, c = flip(me.l, fl), flip(me.x, fx), flip(me.c, fc)
                    spot = 4 * l + 2 * x + c
                    mail.take(vec_all.at[me.h, spot], at(me.h, l, x, c), vec_slot(spot))
    for dh in range(1, planes):
        mail.post(vec_all.at[me.h], vec_all.at[me.h], at(shift(me.h, dh, planes), me.l, me.x, me.c), z_slot(me.h))
    for dh in range(1, planes):
        h = shift(me.h, dh, planes)
        mail.take(vec_all.at[h], at(h, me.l, me.x, me.c), z_slot(h))
    for dh in range(planes):
        for fl in (0, 1):
            h, l = shift(me.h, dh, planes), flip(me.l, fl)
            mail.take(weights.at[2 * h + l], at(h, l, me.x, me.l), w_slot(2 * h + l), mine if dh + fl == 0 else None)
    other = flip(me.c, 1)
    mail.take(chip_in.at[other], sibling(me), r_slot)
    mail.take(chip_cot.at[other], sibling(me), r_slot + 1)
    mail.drain()


def rows_body(me, mail, ins, outs):
    (block,), (rows,) = ins, outs
    greet(plane_peers(me))
    mine = me.l == me.c

    def keep():
        rows[me.t] = block[...]

    for fl in (0, 1):
        for fx in (0, 1):
            local = fl + fx == 0
            mail.post(block, rows.at[me.t], at(me.h, flip(me.l, fl), flip(me.x, fx), me.l), me.t,
                      mine if local else None, keep if local else None)
    for fx in (0, 1):
        for fc in (0, 1):
            x, c = flip(me.x, fx), flip(me.c, fc)
            mail.take(rows.at[2 * x + c], at(me.h, me.c, x, c), 2 * x + c, mine if fx + fc == 0 else None)
    mail.drain()


def run_seat(me, run):
    return at(run // 2, me.l, me.x, run % 2)


def edges(me, mail, pairs, left_slot, right_slot):
    last = 2 * me.planes - 1
    has_left, has_right = me.run > 0, me.run < last
    left, right = run_seat(me, jnp.maximum(me.run - 1, 0)), run_seat(me, jnp.minimum(me.run + 1, last))
    barrier = pltpu.get_barrier_semaphore()
    for has, peer in ((has_left, left), (has_right, right)):
        @pl.when(has)
        def _(peer=peer):
            pl.semaphore_signal(barrier, inc=1, device_id=peer, device_id_type=pl.DeviceIdType.MESH)
    pl.semaphore_wait(barrier, jnp.where(has_left, 1, 0) + jnp.where(has_right, 1, 0))
    (to_left, land_left), (to_right, land_right) = pairs
    mail.post(to_left, land_left, left, 1, jnp.logical_not(has_left))
    mail.post(to_right, land_right, right, 0, jnp.logical_not(has_right))
    for has, slot in ((has_left, left_slot), (has_right, right_slot)):
        @pl.when(jnp.logical_not(has))
        def _(slot=slot):
            slot[...] = jnp.zeros(slot.shape, slot.dtype)
    return has_left, has_right, left, right


def halo_body(me, mail, ins, outs):
    (own,), (ext,) = ins, outs
    pairs = ((own, ext.at[2]), (own, ext.at[0]))
    has_left, has_right, left, right = edges(me, mail, pairs, ext.at[0], ext.at[2])
    ext[1] = own[...]
    mail.take(ext.at[0], left, 0, jnp.logical_not(has_left))
    mail.take(ext.at[2], right, 1, jnp.logical_not(has_right))
    mail.drain()


def rims_body(me, mail, ins, outs):
    (rim,), (got,) = ins, outs
    pairs = ((rim.at[0], got.at[1]), (rim.at[1], got.at[0]))
    has_left, has_right, left, right = edges(me, mail, pairs, got.at[0], got.at[1])
    mail.take(got.at[0], left, 0, jnp.logical_not(has_left))
    mail.take(got.at[1], right, 1, jnp.logical_not(has_right))
    mail.drain()


def swap_body(outward, me, mail, ins, outs):
    (parts,), (got,) = ins, outs
    mine = me.l == me.c
    barrier = pltpu.get_barrier_semaphore()
    cross = at(me.h, me.c, me.x, me.l)
    pl.semaphore_signal(barrier, inc=1, device_id=at(me.h, me.c, flip(me.x, 1), me.l), device_id_type=pl.DeviceIdType.MESH)

    @pl.when(jnp.logical_not(mine))
    def _():
        pl.semaphore_signal(barrier, inc=1, device_id=cross, device_id_type=pl.DeviceIdType.MESH)

    pl.semaphore_wait(barrier, jnp.where(mine, 1, 2))
    for fx in (0, 1):
        x = flip(me.x, fx)
        src = parts.at[x] if outward else parts.at[fx]
        dst = got.at[fx] if outward else got.at[me.x]
        slot = fx

        def keep(fx=fx, x=x):
            if outward:
                got[fx] = parts[x]
            else:
                got[me.x] = parts[fx]

        mail.post(src, dst, at(me.h, me.c, x, me.l), slot, mine if fx == 0 else None, keep if fx == 0 else None)
    for fx in (0, 1):
        x = flip(me.x, fx)
        mail.take(got.at[fx] if outward else got.at[x], at(me.h, me.c, x, me.l), fx, mine if fx == 0 else None)
    mail.drain()


def pair_body(me, mail, ins, outs):
    greet([sibling(me)])
    for i, (src, dst) in enumerate(zip(ins, outs)):
        mail.post(src, dst, sibling(me), i)
    for i, dst in enumerate(outs):
        mail.take(dst, sibling(me), i)
    mail.drain()


def return_body(me, mail, ins, outs):
    rows, grads = ins
    got_rows, got_grads = outs
    planes = me.planes
    greet(plane_peers(me) + column_peers(me))
    mine = me.l == me.c
    corner = 2 * me.l + me.x

    def keep_rows():
        got_rows[corner] = rows[me.t]

    def keep_grads():
        got_grads[me.run] = grads[me.d]

    for fx in (0, 1):
        for fc in (0, 1):
            x, c = flip(me.x, fx), flip(me.c, fc)
            local = fx + fc == 0
            mail.post(rows.at[2 * x + c], got_rows.at[corner], at(me.h, me.c, x, c), corner,
                      mine if local else None, keep_rows if local else None)
    for dh in range(planes):
        for fl in (0, 1):
            h, l = shift(me.h, dh, planes), flip(me.l, fl)
            local = dh + fl == 0
            mail.post(grads.at[2 * h + l], got_grads.at[me.run], at(h, l, me.x, me.l), 4 + me.run,
                      mine if local else None, keep_grads if local else None)
    for fl in (0, 1):
        for fx in (0, 1):
            l, x = flip(me.l, fl), flip(me.x, fx)
            mail.take(got_rows.at[2 * l + x], at(me.h, l, x, me.l), 2 * l + x, mine if fl + fx == 0 else None)
    for dh in range(planes):
        for fc in (0, 1):
            h, c = shift(me.h, dh, planes), flip(me.c, fc)
            mail.take(got_grads.at[2 * h + c], at(h, me.c, me.x, c), 4 + 2 * h + c, mine if dh + fc == 0 else None)
    mail.drain()


def owner_plane(kind, planes):
    return kind * planes // 4


def collect_body(me, mail, ins, outs):
    states, vec = ins
    block, got_vec = outs
    planes = me.planes
    block[...] = jnp.zeros(block.shape, block.dtype)
    greet(line_peers(me))
    count = 2 * planes
    for dh in range(planes):
        for fl in (0, 1):
            h, l = shift(me.h, dh, planes), flip(me.l, fl)
            if dh + fl:
                mail.post(vec.at[2 * h + l], got_vec.at[me.d], at(h, l, me.x, me.c), count + me.d)
    got_vec[me.d] = vec[me.d]
    for kind in range(4):
        home = owner_plane(kind, planes)
        for fl in (0, 1):
            l = flip(me.l, fl)

            def keep(kind=kind):
                block[me.d] = states[kind, me.l]

            mail.post(states.at[kind, l], block.at[me.d], at(home, l, me.x, me.c), me.d,
                      (me.h == home) if fl == 0 else None, keep if fl == 0 else None)
    idle = (me.h * 4) % planes != 0
    for dh in range(planes):
        for fl in (0, 1):
            h, l = shift(me.h, dh, planes), flip(me.l, fl)
            if dh + fl:
                mail.take(block.at[2 * h + l], at(h, l, me.x, me.c), 2 * h + l, idle)
                mail.take(got_vec.at[2 * h + l], at(h, l, me.x, me.c), count + 2 * h + l)
    mail.drain()


def spots(me):
    for fl in (0, 1):
        for fx in (0, 1):
            for fc in (0, 1):
                if fl + fx + fc:
                    l, x, c = flip(me.l, fl), flip(me.x, fx), flip(me.c, fc)
                    yield 4 * l + 2 * x + c, at(me.h, l, x, c)


def scatter_body(me, mail, ins, outs):
    terms, vec = ins
    got, got_vec = outs
    greet(plane_peers(me))
    for spot, seat in spots(me):
        mail.post(terms.at[spot], got.at[me.spot], seat, me.spot)
    for fx in (0, 1):
        for fc in (0, 1):
            if fx + fc:
                x, c = flip(me.x, fx), flip(me.c, fc)
                mail.post(vec.at[2 * x + c], got_vec.at[me.t], at(me.h, me.l, x, c), 8 + me.t)
    got[me.spot] = terms[me.spot]
    got_vec[me.t] = vec[me.t]
    for spot, seat in spots(me):
        mail.take(got.at[spot], seat, spot)
    for fx in (0, 1):
        for fc in (0, 1):
            if fx + fc:
                x, c = flip(me.x, fx), flip(me.c, fc)
                mail.take(got_vec.at[2 * x + c], at(me.h, me.l, x, c), 8 + 2 * x + c)
    mail.drain()


def share_body(me, mail, ins, outs):
    (block,), (got,) = ins, outs
    greet(plane_peers(me))
    for spot, seat in spots(me):
        mail.post(block, got.at[me.spot], seat, me.spot)
    got[me.spot] = block[...]
    for spot, seat in spots(me):
        mail.take(got.at[spot], seat, spot)
    mail.drain()


def deliver_body(me, mail, ins, outs):
    (blocks,), (got,) = ins, outs
    planes = me.planes
    greet(line_peers(me))
    kind = me.h * 4 // planes
    idle = (me.h * 4) % planes != 0
    for dh in range(planes):
        for fl in (0, 1):
            h, l = shift(me.h, dh, planes), flip(me.l, fl)
            if dh + fl:
                mail.post(blocks.at[2 * h + l], got.at[kind, me.l], at(h, l, me.x, me.c), 2 * kind + me.l, idle)

    @pl.when(jnp.logical_not(idle))
    def _():
        got[kind, me.l] = blocks[me.d]

    for other in range(4):
        home = owner_plane(other, planes)
        for fl in (0, 1):
            l = flip(me.l, fl)
            mail.take(got.at[other, l], at(home, l, me.x, me.c), 2 * other + l, (me.h == home) if fl == 0 else None)
    mail.drain()


def normalize(values_in):
    center = values_in - jnp.mean(values_in, axis=-1, keepdims=True)
    inverse = lax.rsqrt(jnp.mean(center * center, axis=-1, keepdims=True) + norm_epsilon)
    return (center * inverse, inverse)


def norm_back(grad_rows, unit, inverse, gain):
    scaled = grad_rows * gain
    return inverse * (
        scaled
        - jnp.mean(scaled, axis=-1, keepdims=True)
        - unit * jnp.mean(scaled * unit, axis=-1, keepdims=True)
    )


def gelu_value(pre):
    return pre * 0.5 * (1.0 + lax.erf(pre * root_half))


def gelu_slope(pre):
    return 0.5 * (1.0 + lax.erf(pre * root_half)) + pre * jnp.exp(-0.5 * pre * pre) * gauss_factor


def narrow(value):
    return value.astype(jnp.bfloat16)


def wide(value):
    return value.astype(jnp.float32)


def mul(left, right):
    return jnp.dot(left, right, preferred_element_type=jnp.float32)


def orthogonalize(gram, block):
    norm = jnp.sqrt(jnp.trace(gram)) + frobenius_epsilon
    gram = narrow(gram / (norm * norm))
    state = narrow(wide(block) / norm)
    for sweep in range(NS_STEPS):
        poly = narrow(quintic_two * wide(gram) + quintic_three * mul(gram, gram))
        state = narrow(quintic_one * wide(state) + mul(poly, state))
        if sweep < NS_STEPS - 1:
            half = narrow(quintic_one * wide(gram) + mul(poly, gram))
            gram = narrow(quintic_one * wide(half) + mul(half, poly))
    return state


def head_slots(values, heads, offset):
    grid = values.reshape(values.shape[0], heads, HDIM)
    return jnp.pad(grid, ((0, 0), (0, 0), (offset, LANES - HDIM - offset))).reshape(values.shape[0], heads * LANES)


def halves(matrix, room):
    rows, cols = matrix.shape
    grid = narrow(matrix).reshape(rows, 2, cols // 2).transpose(1, 0, 2)
    return jnp.pad(grid, ((0, 0), (0, 0), (0, room - cols // 2)))


def whole(pair, cols):
    return pair[:, :, : cols // 2].transpose(1, 0, 2).reshape(pair.shape[1], cols)


def local(
    inputs,
    cotangent,
    clip_lengths,
    inward_weight,
    outward_weight,
    expand_weight,
    shrink_weight,
    gains,
    shifts,
    biases,
    expand_bias,
    inward_moment,
    outward_moment,
    expand_moment,
    shrink_moment,
    gains_moment,
    shifts_moment,
    biases_moment,
    expand_bias_moment,
):
    data_count = lax.axis_size("dp")
    tensor_count = lax.axis_size("tensor")
    devices = data_count * tensor_count
    planes = data_count // 2
    assert tensor_count == 4 and planes % 4 == 0
    data_at = lax.axis_index("dp")
    tensor_at = lax.axis_index("tensor")
    plane_at, level = data_at // 2, data_at % 2
    column, core = tensor_at // 2, tensor_at % 2
    rows, width = inputs.shape
    run = rows * tensor_count
    assert run >= MAXCLIP
    chip = 2 * rows
    run_at = 2 * plane_at + core
    shard = inward_weight.shape[0]
    head_cols = inward_weight.shape[2]
    heads = head_cols // HDIM
    slots = heads * LANES
    hidden = expand_weight.shape[1]
    hidden_width = hidden * tensor_count
    group = 2 * column + level
    twin = (tensor_at + 2) % tensor_count
    piece = width // devices
    hidden_piece = hidden_width // devices
    vec_size = 8 * piece + hidden_piece
    scale = 1.0 / math.sqrt(HDIM)
    to_twin = [(i, (i + 2) % tensor_count) for i in range(tensor_count)]

    def talk(body, name, number, arrays, outs, sends, recvs):
        return call(body, name, number, data_count, arrays, outs, sends, recvs)

    def gather_weights(packed):
        mine = lax.all_gather(packed, "dp", axis=0, tiled=True)
        return mine, lax.ppermute(mine, "tensor", to_twin)

    packed_vec = jnp.concatenate([gains.reshape(-1), shifts.reshape(-1), biases.reshape(-1), expand_bias])
    packed_vec = jnp.pad(packed_vec, (0, 1024 - vec_size)).reshape(8, LANES)
    section = narrow(inward_weight).reshape(shard, 3, heads, HDIM)
    blank = jnp.zeros((shard, heads, HDIM), jnp.bfloat16)
    inward_packed = jnp.concatenate(
        [
            jnp.concatenate([section[:, 0], blank], axis=2).reshape(shard, slots),
            jnp.concatenate([section[:, 1], section[:, 2]], axis=2).reshape(shard, slots),
        ],
        axis=1,
    )
    vec_all, inward_full, chip_in, chip_cot = talk(
        begin_body,
        "begin",
        1,
        (packed_vec, inward_packed, inputs, cotangent),
        (
            ((planes, 8, 8, LANES), jnp.float32),
            ((data_count, shard, 2 * slots), jnp.bfloat16),
            ((2, rows, width), jnp.float32),
            ((2, rows, width), jnp.float32),
        ),
        7 + 2 * planes + 2 + planes - 1,
        8 + 3 * planes + 2,
    )
    table = vec_all.reshape(devices, 1024)

    def spread(first, count, size):
        return table[:, first : first + count * size].reshape(devices, count, size).transpose(1, 0, 2).reshape(count, -1)

    full_gains = spread(0, 2, piece)
    full_shifts = spread(2 * piece, 2, piece)
    full_biases = spread(4 * piece, 4, piece)
    full_hidden = spread(8 * piece, 1, hidden_piece)[0]
    chip_in = chip_in.reshape(chip, width)
    chip_cot = chip_cot.reshape(chip, width)
    inward_full = inward_full.reshape(width, 2 * slots)
    query_w, pair_w = inward_full[:, :slots], inward_full[:, slots:]

    unit_one, inverse_one = normalize(inputs)
    normed_one = narrow(unit_one * full_gains[0] + full_shifts[0])
    (rows_run,) = talk(rows_body, "rows", 2, (normed_one,), (((4, rows, width), jnp.bfloat16),), 4, 4)
    rows_run = rows_run.reshape(run, width)
    up_shard = jnp.concatenate([narrow(expand_weight), narrow(outward_weight).T], axis=1)
    up_mine, up_twin = gather_weights(up_shard)
    down_mine, down_twin = gather_weights(narrow(shrink_weight).T)

    def group_slice(row):
        return lax.dynamic_slice_in_dim(row, group * head_cols, head_cols)[None]

    query_bias = head_slots(group_slice(full_biases[0]), heads, 0)
    pair_bias = head_slots(group_slice(full_biases[1]), heads, HDIM)
    query = narrow(mul(rows_run, query_w) + query_bias) * jnp.bfloat16(scale)
    pairs = narrow(mul(rows_run, pair_w) + pair_bias)
    (extended,) = talk(halo_body, "halo", 3, (pairs,), (((3, run, slots), jnp.bfloat16),), 2, 2)
    extended = extended.reshape(3 * run, slots)
    base = (run_at * run).astype(jnp.int32).reshape(1)
    attended, log_totals = attend_forward(clip_lengths, base, query, extended, heads, 768, 512)
    (attended_chip,) = talk(
        functools.partial(swap_body, True), "swap_out", 4, (attended.reshape(2, chip, head_cols),),
        (((2, chip, head_cols), jnp.bfloat16),), 2, 2,
    )

    out_mine, out_twin = up_mine[:, hidden:], up_twin[:, hidden:]
    expand_mine, expand_twin = up_mine[:, :hidden], up_twin[:, :hidden]
    out_part = narrow(over_last(attended_chip[0], out_mine) + over_last(attended_chip[1], out_twin))
    (out_other,) = talk(pair_body, "pair_mid", 5, (out_part,), (((chip, width), jnp.bfloat16),), 1, 1)
    mid = chip_in + (wide(out_part) + wide(out_other)) + full_biases[2]
    unit_two, inverse_two = normalize(mid)
    rows_two = narrow(unit_two * full_gains[1] + full_shifts[1])
    grad_b = narrow(chip_cot)
    hidden_mine = lax.dynamic_slice_in_dim(full_hidden, tensor_at * hidden, hidden)
    hidden_twin = lax.dynamic_slice_in_dim(full_hidden, twin * hidden, hidden)

    def feed(expand_w, shrink_w, bias):
        pre = mul(rows_two, expand_w) + bias
        act = narrow(gelu_value(pre))
        pre_grad = mul(grad_b, shrink_w) * gelu_slope(pre)
        return act, narrow(pre_grad), jnp.sum(pre_grad, axis=0)

    act_mine, pre_mine, hidden_sum_mine = feed(expand_mine, down_mine, hidden_mine)
    act_twin, pre_twin, hidden_sum_twin = feed(expand_twin, down_twin, hidden_twin)
    feed_part = narrow(over_last(act_mine, down_mine) + over_last(act_twin, down_twin))
    back_part = narrow(over_last(pre_mine, expand_mine) + over_last(pre_twin, expand_twin))
    feed_away = lax.dynamic_slice_in_dim(feed_part, (1 - core) * rows, rows, 0)
    feed_home = lax.dynamic_slice_in_dim(feed_part, core * rows, rows, 0)
    feed_other, back_other = talk(
        pair_body, "pair_feed", 6, (feed_away, back_part),
        (((rows, width), jnp.bfloat16), ((chip, width), jnp.bfloat16)), 2, 2,
    )
    output = (
        lax.dynamic_slice_in_dim(mid, core * rows, rows, 0) + (wide(feed_home) + wide(feed_other)) + full_biases[3]
    )
    normed_two_grad = wide(back_part) + wide(back_other)
    mid_grad = chip_cot + norm_back(normed_two_grad, unit_two, inverse_two, full_gains[1])
    mid_grad_b = narrow(mid_grad)

    def reduce_over(mine, away):
        got = lax.ppermute(narrow(away), "tensor", to_twin)
        return wide(lax.psum_scatter(narrow(mine + wide(got)), "dp", scatter_dimension=0, tiled=True))

    shrink_shard = reduce_over(over_first(grad_b, act_mine), over_first(grad_b, act_twin))
    expand_shard = reduce_over(over_first(rows_two, pre_mine), over_first(rows_two, pre_twin))
    outward_shard = reduce_over(
        over_first(mid_grad_b, attended_chip[0]), over_first(mid_grad_b, attended_chip[1])
    )

    attended_grad = jnp.stack([narrow(mul(mid_grad_b, out_mine)), narrow(mul(mid_grad_b, out_twin))])
    (attended_grad,) = talk(
        functools.partial(swap_body, False), "swap_back", 7, (attended_grad,),
        (((2, chip, head_cols), jnp.bfloat16),), 2, 2,
    )
    query_grad, pair_own, rims, _ = attend_backward(
        clip_lengths, base, query, extended, attended, attended_grad.reshape(run, head_cols), log_totals, heads, 256, 512
    )
    (arrived,) = talk(rims_body, "rims", 8, (rims,), (((2, run, slots), jnp.bfloat16),), 2, 2)
    pair_grad = pair_own + wide(arrived[0]) + wide(arrived[1])
    pair_grad_b = narrow(pair_grad)
    row_terms = narrow(over_last(query_grad, query_w) + over_last(pair_grad_b, pair_w))
    inward_terms = jnp.concatenate(
        [narrow(over_first(rows_run, query_grad)), narrow(over_first(rows_run, pair_grad_b))], axis=1
    )
    got_rows, got_inward = talk(
        return_body, "give_back", 9,
        (row_terms.reshape(4, rows, width), inward_terms.reshape(data_count, shard, 2 * slots)),
        (((4, rows, width), jnp.bfloat16), ((data_count, shard, 2 * slots), jnp.bfloat16)),
        4 + 2 * planes, 4 + 2 * planes,
    )
    normed_one_grad = jnp.sum(wide(got_rows), axis=0)
    inward_sum = jnp.sum(wide(got_inward), axis=0)
    mid_grad_own = lax.dynamic_slice_in_dim(mid_grad, core * rows, rows, 0)
    input_grad = mid_grad_own + norm_back(normed_one_grad, unit_one, inverse_one, full_gains[0])
    grid = inward_sum.reshape(shard, 2, heads, LANES)
    inward_grad = jnp.stack(
        [
            grid[:, 0, :, :HDIM].reshape(shard, head_cols),
            grid[:, 1, :, :HDIM].reshape(shard, head_cols),
            grid[:, 1, :, HDIM:].reshape(shard, head_cols),
        ],
        axis=1,
    )

    def placed(row, first, size):
        return lax.dynamic_update_slice_in_dim(jnp.zeros((size,), jnp.float32), row, first, 0)

    query_sum = jnp.sum(wide(query_grad), axis=0).reshape(heads, LANES)[:, :HDIM].reshape(-1)
    value_sum = jnp.sum(pair_grad, axis=0).reshape(heads, LANES)[:, HDIM:].reshape(-1)
    vec_terms = jnp.stack(
        [
            jnp.sum(normed_one_grad * unit_one, axis=0),
            0.5 * jnp.sum(normed_two_grad * unit_two, axis=0),
            jnp.sum(normed_one_grad, axis=0),
            0.5 * jnp.sum(normed_two_grad, axis=0),
            placed(query_sum, group * head_cols, width),
            placed(value_sum, group * head_cols, width),
            0.5 * jnp.sum(mid_grad, axis=0),
            jnp.sum(cotangent, axis=0),
        ]
    )
    hidden_terms = placed(hidden_sum_mine, tensor_at * hidden, hidden_width) + placed(
        hidden_sum_twin, twin * hidden, hidden_width
    )
    vec_terms = jnp.concatenate(
        [vec_terms.reshape(8, devices, piece).transpose(1, 0, 2).reshape(devices, 8 * piece),
         hidden_terms.reshape(devices, hidden_piece)],
        axis=1,
    )
    vec_terms = jnp.pad(vec_terms, ((0, 0), (0, 1024 - vec_size))).reshape(data_count, 4, 8, LANES)

    outward_turned = outward_shard.T
    shrink_turned = shrink_shard.T
    inward_state = momentum_decay * inward_moment + inward_grad
    outward_state = momentum_decay * outward_moment + outward_turned
    expand_state = momentum_decay * expand_moment + expand_shard
    shrink_state = momentum_decay * shrink_moment + shrink_turned
    room = hidden // 2
    states = jnp.stack(
        [
            halves(inward_state.reshape(shard, 3 * head_cols), room),
            halves(outward_state.T, room),
            halves(expand_state, room),
            halves(shrink_state.T, room),
        ]
    )
    block, got_vec = talk(
        collect_body, "collect", 10, (states, vec_terms),
        (((data_count, shard, room), jnp.bfloat16), ((data_count, 4, 8, LANES), jnp.float32)),
        2 * planes - 1 + 8, 4 * planes,
    )
    block = block.reshape(width, room)
    gram_terms = narrow(over_last(block, block)).reshape(8, width // 8, width)
    got_gram, got_vec = talk(
        scatter_body, "gram_sum", 11, (gram_terms, jnp.sum(got_vec, axis=0)),
        (((8, width // 8, width), jnp.bfloat16), ((4, 8, LANES), jnp.float32)), 10, 12,
    )
    (gram,) = talk(
        share_body, "gram_share", 12, (narrow(jnp.sum(wide(got_gram), axis=0)),),
        (((8, width // 8, width), jnp.bfloat16),), 7, 8,
    )
    ortho = orthogonalize(wide(gram.reshape(width, width)), block)
    (mine,) = talk(
        deliver_body, "deliver", 13, (ortho.reshape(data_count, shard, room),),
        (((4, 2, shard, room), jnp.bfloat16),), 2 * planes - 1, 8,
    )
    ortho_in = wide(whole(mine[0], 3 * head_cols)).reshape(inward_weight.shape)
    ortho_out = wide(whole(mine[1], head_cols)).T
    ortho_up = wide(whole(mine[2], hidden))
    ortho_down = wide(whole(mine[3], hidden)).T
    inward_new = inward_weight - learn_rate * 0.2 * math.sqrt(3 * width) * ortho_in
    outward_new = outward_weight - learn_rate * 0.2 * math.sqrt(width) * ortho_out
    expand_new = expand_weight - learn_rate * 0.2 * math.sqrt(max(width, hidden_width)) * ortho_up
    shrink_new = shrink_weight - learn_rate * 0.2 * math.sqrt(max(width, hidden_width)) * ortho_down

    vec = jnp.sum(got_vec, axis=0).reshape(-1)
    gains_grad = vec[: 2 * piece].reshape(2, piece)
    shifts_grad = vec[2 * piece : 4 * piece].reshape(2, piece)
    biases_grad = vec[4 * piece : 8 * piece].reshape(4, piece)
    expand_bias_grad = vec[8 * piece : vec_size]
    gains_state = momentum_decay * gains_moment + gains_grad
    shifts_state = momentum_decay * shifts_moment + shifts_grad
    biases_state = momentum_decay * biases_moment + biases_grad
    expand_bias_state = momentum_decay * expand_bias_moment + expand_bias_grad
    gains_new = gains - vector_rate * gains_state
    shifts_new = shifts - vector_rate * shifts_state
    biases_new = biases - vector_rate * biases_state
    expand_bias_new = expand_bias - vector_rate * expand_bias_state
    return (
        output,
        input_grad,
        inward_grad,
        outward_turned,
        expand_shard,
        shrink_turned,
        gains_grad,
        shifts_grad,
        biases_grad,
        expand_bias_grad,
        inward_new,
        outward_new,
        expand_new,
        shrink_new,
        gains_new,
        shifts_new,
        biases_new,
        expand_bias_new,
        inward_state,
        outward_state,
        expand_state,
        shrink_state,
        gains_state,
        shifts_state,
        biases_state,
        expand_bias_state,
    )


def solution(mesh):
    in_specs = (
        P(("dp", "tensor"), None),
        P(("dp", "tensor"), None),
        P(),
        P("dp", None, "tensor"),
        P("tensor", "dp"),
        P("dp", "tensor"),
        P("tensor", "dp"),
        P(None, ("dp", "tensor")),
        P(None, ("dp", "tensor")),
        P(None, ("dp", "tensor")),
        P(("dp", "tensor")),
        P("dp", None, "tensor"),
        P("tensor", "dp"),
        P("dp", "tensor"),
        P("tensor", "dp"),
        P(None, ("dp", "tensor")),
        P(None, ("dp", "tensor")),
        P(None, ("dp", "tensor")),
        P(("dp", "tensor")),
    )
    out_specs = (
        P(("dp", "tensor"), None),
        P(("dp", "tensor"), None),
        P("dp", None, "tensor"),
        P("tensor", "dp"),
        P("dp", "tensor"),
        P("tensor", "dp"),
        P(None, ("dp", "tensor")),
        P(None, ("dp", "tensor")),
        P(None, ("dp", "tensor")),
        P(("dp", "tensor")),
        P("dp", None, "tensor"),
        P("tensor", "dp"),
        P("dp", "tensor"),
        P("tensor", "dp"),
        P(None, ("dp", "tensor")),
        P(None, ("dp", "tensor")),
        P(None, ("dp", "tensor")),
        P(("dp", "tensor")),
        P("dp", None, "tensor"),
        P("tensor", "dp"),
        P("dp", "tensor"),
        P("tensor", "dp"),
        P(None, ("dp", "tensor")),
        P(None, ("dp", "tensor")),
        P(None, ("dp", "tensor")),
        P(("dp", "tensor")),
    )
    return jax.shard_map(local, mesh=mesh, in_specs=in_specs, out_specs=out_specs, check_vma=False)
```

time: 1980 us -> 736 us (0.37)
  waiting for transfers between devices: 671 us -> 125 us
  Pallas kernels: 0 us -> 353 us
  blocking collectives: 301 us -> 0 us
  matrix products: 364 us -> 78.4 us
  local copies, waits for them, and re-layouts: 334 us -> 86.2 us
  other arithmetic: 241 us -> 62.6 us
    pallas_call x0 -> x15, Pallas kernels: none -> 353 us  [the longest x13 302 us: call(): pl.pallas_call(kernel, out_shape=tuple((jax.ShapeDtypeStruct(*o) for o in...]
    dot_general x86 -> x34, matrix products: 360 us -> 78.4 us  [the longest x17 31.2 us: mul(): return jnp.dot(left, right, preferred_element_type=jnp.float32)]
    all_gather x10 -> x2, waiting for transfers between devices: 245 us -> 0.01 us  [gather_weights(): mine = lax.all_gather(packed, 'dp', axis=0, tiled=True)]
    all_gather x5 -> x0, blocking collectives: 221 us -> none  [the longest x1 69.1 us: local(): lax.all_gather(outward_weight.astype(jnp.bfloat16), 'dp', axis=1, tiled=T...]
    psum x1 -> x0, waiting for transfers between devices: 177 us -> none  [from_root(): return lax.psum(kept, axis)]
    cond x2 -> x0, other arithmetic: 104 us -> none
    reduce_scatter x7 -> x2, waiting for transfers between devices: 211 us -> 125 us  [reduce_over(): lax.psum_scatter(narrow(mine + wide(got)), 'dp', scatter_dimension=0, til...]
    unnamed x2 -> x0, blocking collectives: 79.6 us -> none
  transfers between devices with their start and end apart: 23 -> 10, of which waited for: 12 -> 2; matrix products, arithmetic and copies ran while one was open for 39% -> 20% of each run, Pallas kernels for 0% -> 28%
where the time goes in v1:
time: 736 us; the launch traced here: 727 us
  Pallas kernels  353 us (48%)
  waiting for transfers between devices  125 us (17%)
  local copies, waits for them, and re-layouts  86.2 us (12%)
  matrix products  78.4 us (11%)
  other arithmetic  62.6 us (9%)
  between operations  16.1 us (2%)
    pallas_call x13, Pallas kernels, call(): pl.pallas_call(kernel, out_shape=tuple((jax.ShapeDtypeStruct(*o) for o in...  302 us
    reduce_scatter x2, waiting for transfers between devices, reduce_over(): lax.psum_scatter(narrow(mine + wide(got)), 'dp', scatter_dimension=0, til...  125 us
    dot_general x17, matrix products, mul(): return jnp.dot(left, right, preferred_element_type=jnp.float32)  31.2 us
    pallas_call x1, Pallas kernels, attend_backward(): pl.pallas_call(functools.partial(backward_body, heads, bq, bk, clips.shap...  30.9 us
    unnamed x191, local copies, waits for them, and re-layouts  25.6 us
    dot_general x9, matrix products, over_last(): lax.dot_general(left, right, (((1,), (1,)), ((), ())), preferred_element_...  25 us
    dot_general x8, matrix products, over_first(): lax.dot_general(left, right, (((0,), (0,)), ((), ())), preferred_element_...  22.2 us
    pallas_call x1, Pallas kernels, attend_forward(): pl.pallas_call(functools.partial(forward_body, heads, bq, bk, clips.shape...  21 us
  transfers between devices with their start and end apart: 10, of which 2 were waited for; matrix products, arithmetic and copies ran while one was open for 20% of the time, Pallas kernels for 28%

profile of v1, /device:TPU:0, one launch (start us, length us, event | category | flops | bytes accessed | tf_op | source)
XLA Modules:
  0.0 726.8 jit_solution(13598789075859835489)
XLA Ops:
  13.0 46.5 %begin.1 = (f32[4,8,8,128]{3,2,1,0:T(8,128)}, bf16[8,96,768]{2,1,0:T(8,128)(2,1)}, f32[2,384,768]{2,1,0:T(8,128)}, f32[2,384,768]{2,1,0:T(8,128)}) custom-call(f32[8,128]{1,0:T(8,128)} %fusion.71.refs_0_, bf16[96,768]{1,0:T(8,128)(2,1)} %pad_maximum_fusion.5.refs_1_, f32[384,768]{1,0:T(8,128)} %refs_2_.1, f32[384,768]{1,0:T(8,128)} %refs_3_.1), custom_call_target="tpu_custom_call" | custom-call | tf_op jit(solution)/shard_map/begin/pallas_call | solution.py:315
  65.7 29.7 %rows.1 = bf16[4,384,768]{2,1,0:T(8,128)(2,1)} custom-call(bf16[384,768]{1,0:T(8,128)(2,1)} %add_convert_fusion.10.refs_0_), custom_call_target="tpu_custom_call" | custom-call | tf_op jit(solution)/shard_map/rows/pallas_call | solution.py:315
  96.0 2.8 copy.209
  99.6 3.5 fusion.1.refs_0_
  103.1 7.7 %halo.1 = bf16[3,1536,384]{2,1,0:T(8,128)(2,1)} custom-call(bf16[1536,384]{1,0:T(8,128)(2,1)} %fusion.1.refs_0_), custom_call_target="tpu_custom_call" | custom-call | tf_op jit(solution)/shard_map/halo/pallas_call | solution.py:315
  115.5 3.5 fusion.2.q_ref
  119.0 21.0 %attend_forward.1 = (bf16[1536,192]{1,0:T(8,128)(2,1)}, f32[8,1536]{1,0:T(8,128)}) custom-call(s32[12]{0:T(128)} %clips_ref.3, s32[1]{0:T(128)} %bitcast.8.base_ref, bf16[1536,384]{1,0:T(8,128)(2,1)} %fusion.2.q_ref, bf16[4608,384]{1,0:T(8,128)(2,1)} %bitcast.206), custom_call_target="tpu_custom_call" | custom-call | tf_op jit(solution)/shard_map/attend_forward/pallas_call | solution.py:185
  139.9 10.5 %swap_out.1 = bf16[2,768,192]{2,1,0:T(8,128)(2,1)} custom-call(bf16[2,768,192]{2,1,0:T(8,128)(2,1)} %bitcast.211), custom_call_target="tpu_custom_call" | custom-call | tf_op jit(solution)/shard_map/swap_out/pallas_call | solution.py:315
  166.9 2.5 add_convert_fusion.9.refs_0_
  169.3 36.6 %pair_mid.1 = bf16[768,768]{1,0:T(8,128)(2,1)} custom-call(bf16[768,768]{1,0:T(8,128)(2,1)} %add_convert_fusion.9.refs_0_), custom_call_target="tpu_custom_call" | custom-call | tf_op jit(solution)/shard_map/pair_mid/pallas_call | solution.py:315
  206.0 2.9 fusion.79
  213.5 2.8 multiply_convert_fusion
  216.3 2.8 add_convert_fusion.7
  221.1 3.6 fusion.89
  224.7 2.8 fusion.88
  228.6 3.4 add_convert_fusion.6.refs_1_
  232.0 6.4 pair_feed.1
  238.5 3.6 multiply_reduce_fusion
  249.5 9.9 %swap_back.1 = bf16[2,768,192]{2,1,0:T(8,128)(2,1)} custom-call(bf16[2,768,192]{2,1,0:T(8,128)(2,1)} %pad_maximum_fusion.1.refs_0_), custom_call_target="tpu_custom_call" | custom-call | tf_op jit(solution)/shard_map/swap_back/pallas_call | solution.py:315
  259.4 30.9 %attend_backward.1 = (bf16[1536,384]{1,0:T(8,128)(2,1)}, f32[1536,384]{1,0:T(8,128)}, bf16[2,1536,384]{2,1,0:T(8,128)(2,1)}, f32[8,384]{1,0:T(8,128)}) custom-call(s32[12]{0:T(128)} %clips_ref.3, s32[1]{0:T(128)} %bitcast.8.base_ref, bf16[1536,384]{1,0:T(8,128)(2,1)} %fusion.2.q_ref, bf16[4608,384]{1,0:T(8,128)(2,1)} %bitcast.207, ...), custom_call_target="tpu_custom_call" | custom-call | tf_op jit(solution)/shard_map/attend_backward/pallas_call | solution.py:197
  290.3 4.1 convolution_convert_fusion.4
  294.5 3.6 fusion.51
  298.1 2.2 convolution_convert_fusion.1
  301.4 31.1 %rims.1 = bf16[2,1536,384]{2,1,0:T(8,128)(2,1)} custom-call(bf16[2,1536,384]{2,1,0:T(8,128)(2,1)} %get-tuple-element.53.refs_0_), custom_call_target="tpu_custom_call" | custom-call | tf_op jit(solution)/shard_map/rims/pallas_call | solution.py:315
  332.5 3.6 fusion.39
  338.8 2.4 copy.216
  343.2 5.8 add_convert_fusion
  348.9 49.7 %give_back.1 = (bf16[4,384,768]{2,1,0:T(8,128)(2,1)}, bf16[8,96,768]{2,1,0:T(8,128)(2,1)}) custom-call(bf16[4,384,768]{2,1,0:T(8,128)(2,1)} %bitcast.208, bf16[8,96,768]{2,1,0:T(8,128)(2,1)} %bitcast.209), custom_call_target="tpu_custom_call" | custom-call | tf_op jit(solution)/shard_map/give_back/pallas_call | solution.py:315
  398.7 3.9 convolution_convert_fusion.2
  402.6 2.1 add_convert_fusion.11
  406.9 3.9 convert_reduce_fusion
  410.8 3.4 add_convert_fusion.4
  414.9 2.4 multiply_reduce_fusion.3
  419.5 2.0 convert_reduce_fusion.2
  457.7 4.1 add_convert_fusion.5
  461.8 2.2 convert_reduce_fusion.3
  465.8 2.1 fusion.81
  482.0 2.6 add_add_fusion
  487.9 59.7 %reduce-scatter.8.cloned.1.call-done = bf16[96,768]{1,0:T(8,128)(2,1)} async-done(((bf16[768,768]{1,0:T(8,128)(2,1)}), bf16[96,768]{1,0:T(8,128)(2,1)}) %reduce-scatter.8.cloned.1.call-update) | async-done | bytes 147472 | tf_op jit(solution)/shard_map/reduce_scatter | solution.py:839
  549.4 65.2 %reduce-scatter.6.cloned.1.call-done = bf16[96,768]{1,0:T(8,128)(2,1)} async-done(((bf16[768,768]{1,0:T(8,128)(2,1)}), bf16[96,768]{1,0:T(8,128)(2,1)}) %reduce-scatter.6.cloned.1.call-update) | async-done | bytes 147472 | tf_op jit(solution)/shard_map/reduce_scatter | solution.py:839
  617.4 18.3 %collect.1 = (bf16[8,96,384]{2,1,0:T(8,128)(2,1)}, f32[8,4,8,128]{3,2,1,0:T(8,128)}) custom-call(bf16[4,2,96,384]{3,2,1,0:T(8,128)(2,1)} %pad_maximum_fusion.2.refs_0_, f32[8,4,8,128]{3,2,1,0:T(8,128)} %bitcast.234), custom_call_target="tpu_custom_call" | custom-call | tf_op jit(solution)/shard_map/collect/pallas_call | solution.py:315
  635.6 3.1 convolution_convert_fusion
  639.3 18.9 %gram_sum.1 = (bf16[8,96,768]{2,1,0:T(8,128)(2,1)}, f32[4,8,128]{2,1,0:T(8,128)}) custom-call(bf16[8,96,768]{2,1,0:T(8,128)(2,1)} %bitcast.210, f32[4,8,128]{2,1,0:T(8,128)} %reduce_sum.240.refs_1_), custom_call_target="tpu_custom_call" | custom-call | tf_op jit(solution)/shard_map/gram_sum/pallas_call | solution.py:315
  658.3 2.1 reduce_sum.242.refs_0_
  660.4 18.0 %gram_share.1 = bf16[8,96,768]{2,1,0:T(8,128)(2,1)} custom-call(bf16[96,768]{1,0:T(8,128)(2,1)} %reduce_sum.242.refs_0_), custom_call_target="tpu_custom_call" | custom-call | tf_op jit(solution)/shard_map/gram_share/pallas_call | solution.py:315
  678.5 2.9 fusion.3
  690.5 2.5 fusion.29
  693.0 18.4 %deliver.1 = bf16[4,2,96,384]{3,2,1,0:T(8,128)(2,1)} custom-call(bf16[8,96,384]{2,1,0:T(8,128)(2,1)} %bitcast.231), custom_call_target="tpu_custom_call" | custom-call | tf_op jit(solution)/shard_map/deliver/pallas_call | solution.py:315
  (355 shorter events, 137.3 us)
Async XLA Ops:
  7.2 3.7 copy-start.35
  7.2 88.8 %all-gather.3.cloned.1.call-start = ((), (), s32[]{:S(2)}) async-start(), calls=%async_computation.3 | async-start | bytes 1769472 | tf_op jit(solution)/shard_map/all_gather | solution.py:737
  10.0 154.4 %all-gather.5.cloned.1.call-start = ((), (), s32[]{:S(2)}) async-start(), calls=%async_computation.4 | async-start | bytes 1327104 | tf_op jit(solution)/shard_map/all_gather | solution.py:737
  10.8 475.3 %reduce-scatter.10.cloned.1.call-start = ((), (), s32[]{:S(2)}) async-start(), calls=%async_computation.7 | async-start | bytes 442368
  13.0 51.1 %copy-start = (f32[384,768]{1,0:T(8,128)S(1)}, f32[384,768]{1,0:T(8,128)}, u32[]{:S(2)}) copy-start(f32[384,768]{1,0:T(8,128)} %refs_2_.1) | copy-start | bytes 3538948
  64.6 30.8 %copy-start.50 = (f32[384]{0:T(512)}, f32[384]{0:T(512)S(1)}, u32[]{:S(2)}) copy-start(f32[384]{0:T(512)S(1)} %add_rsqrt_fusion.1) | copy-start | bytes 4612
  96.0 3.6 copy-start.17
  98.7 68.1 %collective-permute-start = (bf16[768,960]{0,1:T(8,128)(2,1)}, bf16[768,960]{0,1:T(8,128)(2,1)}, u32[]{:S(2)}, u32[]{:S(2)}) collective-permute-start(bf16[768,960]{0,1:T(8,128)(2,1)} %copy.209), channel_id=1, source_target_pairs={{0,2},{1,3},{2,0},{3,1},{4,6},{5,7},{6,4},{7,5},{8,10},{9,11},{10,... | collective-permute-start | bytes 4423688 | tf_op jit(solution)/shard_map/ppermute | solution.py:738
  139.9 23.3 %copy-start.6 = (f32[2,384,768]{2,1,0:T(8,128)S(1)}, f32[2,384,768]{2,1,0:T(8,128)}, u32[]{:S(2)}) copy-start(f32[2,384,768]{2,1,0:T(8,128)} %get-tuple-element.47) | copy-start | bytes 7077892
  154.0 6.6 copy-start.42
  164.4 51.9 %collective-permute-start.1 = (bf16[768,768]{1,0:T(8,128)(2,1)}, bf16[768,768]{1,0:T(8,128)(2,1)}, u32[]{:S(2)}, u32[]{:S(2)}) collective-permute-start(bf16[768,768]{1,0:T(8,128)(2,1)} %all-gather.5.cloned.1.call-done), channel_id=1, source_target_pairs={{0,2},{1,3},{2,0},{3,1},{4,6},{5,7},{6,4},{7,5},{8,10},{9,11},{10,... | collective-permute-start | bytes 3538952 | tf_op jit(solution)/shard_map/ppermute | solution.py:738
  169.3 36.6 %copy-start.54 = (f32[768]{0:T(1024)S(1)}, f32[768]{0:T(1024)}, u32[]{:S(2)}) copy-start(f32[768]{0:T(1024)} %add.307) | copy-start | bytes 9220
  210.1 3.4 copy-start.21
  219.2 5.5 copy-start.31
  224.7 3.9 copy-start.80
  238.4 3.6 copy-start.5
  238.4 3.6 copy-start.7
  238.4 3.6 copy-start.10
  290.3 4.1 copy-start.8
  290.3 4.1 copy-start.20
  294.5 3.6 copy-start.23
  294.5 3.6 copy-start.82
  332.5 3.6 copy-start.18
  341.1 69.7 %collective-permute-start.4 = (bf16[768,768]{1,0:T(8,128)(2,1)}, bf16[768,768]{1,0:T(8,128)(2,1)}, u32[]{:S(2)}, u32[]{:S(2)}) collective-permute-start(bf16[768,768]{1,0:T(8,128)(2,1)} %convolution_convert_fusion.1), channel_id=1, source_target_pairs={{0,2},{1,3},{2,0},{3,1},{4,6},{5,7},{6,4},{7,5},{8,10},{9,11},{10,... | collective-permute-start | bytes 3538952 | tf_op jit(solution)/shard_map/ppermute | solution.py:838
  341.9 60.7 %collective-permute-start.2 = (bf16[768,192]{0,1:T(8,128)(2,1)}, bf16[768,192]{0,1:T(8,128)(2,1)}, u32[]{:S(2)}, u32[]{:S(2)}) collective-permute-start(bf16[768,192]{0,1:T(8,128)(2,1)} %convolution_convert_fusion.7), channel_id=1, source_target_pairs={{0,2},{1,3},{2,0},{3,1},{4,6},{5,7},{6,4},{7,5},{8,10},{9,11},{10,... | collective-permute-start | bytes 884744 | tf_op jit(solution)/shard_map/ppermute | solution.py:838
  398.7 3.9 copy-start.13
  398.7 3.9 copy-start.27
  406.7 140.9 %reduce-scatter.8.cloned.1.call-start = ((), (), s32[]{:S(2)}) async-start(), calls=%async_computation.6 | async-start | bytes 1327104 | tf_op jit(solution)/shard_map/reduce_scatter | solution.py:839
  406.9 3.9 copy-start.24
  406.9 3.9 copy-start.85
  414.3 200.3 %reduce-scatter.6.cloned.1.call-start = ((), (), s32[]{:S(2)}) async-start(), calls=%async_computation.5 | async-start | bytes 1327104 | tf_op jit(solution)/shard_map/reduce_scatter | solution.py:839
  417.3 32.6 %copy-start.40 = (f32[1,32,24]{2,1,0:T(8,128)S(1)}, f32[1,32,24]{2,1,0:T(8,128)}, u32[]{:S(2)}) copy-start(f32[1,32,24]{2,1,0:T(8,128)} %stack.70) | copy-start | bytes 9220
  418.7 3.5 copy-start.59
  418.7 3.5 copy-start.60
  418.7 4.1 copy-start.41
  418.7 39.0 %collective-permute-start.3 = (bf16[768,768]{1,0:T(8,128)(2,1)}, bf16[768,768]{1,0:T(8,128)(2,1)}, u32[]{:S(2)}, u32[]{:S(2)}) collective-permute-start(bf16[768,768]{1,0:T(8,128)(2,1)} %convolution_convert_fusion.2), channel_id=1, source_target_pairs={{0,2},{1,3},{2,0},{3,1},{4,6},{5,7},{6,4},{7,5},{8,10},{9,11},{10,... | collective-permute-start | bytes 3538952 | tf_op jit(solution)/shard_map/ppermute | solution.py:838
  474.9 7.0 copy-start.62
  474.9 7.0 copy-start.61
  475.0 7.0 copy-start.53
  480.3 4.3 copy-start.49
  480.3 4.3 copy-start.52
  484.7 63.0 %copy-start.36 = (f32[768,96]{0,1:T(8,128)S(1)}, f32[768,96]{0,1:T(8,128)}, u32[]{:S(2)}) copy-start(f32[768,96]{0,1:T(8,128)} %param.33) | copy-start | bytes 884740
  486.1 128.5 %copy-start.37 = (f32[96,768]{1,0:T(8,128)S(1)}, f32[96,768]{1,0:T(8,128)}, u32[]{:S(2)}) copy-start(f32[96,768]{1,0:T(8,128)} %param.32) | copy-start | bytes 884740
  549.4 67.0 %copy-start.32 = (bf16[1,2,96,384]{3,2,1,0:T(8,128)(2,1)S(1)}, bf16[1,2,96,384]{3,2,1,0:T(8,128)(2,1)}, u32[]{:S(2)}) copy-start(bf16[1,2,96,384]{3,2,1,0:T(8,128)(2,1)} %pad_bitcast_fusion.1) | copy-start | bytes 442372
  658.2 20.2 %copy-start.56 = (s32[8,96]{1,0:T(8,128)S(1)}, s32[8,96]{1,0:T(8,128)}, u32[]{:S(2)}) copy-start(s32[8,96]{1,0:T(8,128)} %multiply_add_fusion.5) | copy-start | bytes 9220
  678.4 3.6 copy-start.3
  715.5 3.7 copy-start.74
  715.5 3.7 copy-start.75
  (48 other events, 85.0 us)
Sparse Core Ops, SparseCore 0:
  10.8 63.0 all-gather.2
  76.6 49.9 all-gather.4
  406.8 73.7 reduce-scatter.9
  483.9 63.7 reduce-scatter.7
  550.8 63.7 reduce-scatter.5
